TPU v7x, 256 devices: a whole 4x4x8 slice. The times are simulated.
256 devices in a mesh: ctx: 64 (over x, z, core), dp: 4 (over y).
Axes of the slice: x: 4, y: 4, z: 8, core: 2. Of those that a mesh axis runs over, the one named last changes fastest.
Arguments:
- head_input: bfloat16 [65536, 4096], P(('dp', 'ctx')), parts along dimension 0, may hold values from -6 to 6
- gate_input: bfloat16 [65536, 4096], P(('dp', 'ctx')), parts along dimension 0, may hold values from -6 to 6
- write_vector: bfloat16 [65536, 128], P(('dp', 'ctx')), parts along dimension 0, may hold values from -2.5 to 2.5
- read_vector: bfloat16 [65536, 128], P(('dp', 'ctx')), parts along dimension 0, may hold values from -2.5 to 2.5
- increment_preactivation: bfloat16 [65536, 64], P(('dp', 'ctx')), parts along dimension 0, may hold values from -2 to 8
- step_bias: float32 [64], replicated, may hold values from -1 to 0.5
- decay_log: float32 [64], replicated, may hold values from -9.3 to -2.3
- skip_gain: float32 [64], replicated, may hold values from 0.5 to 1.5
- norm_weight: float32 [4096], replicated, may hold values from 0.5 to 1.5
- doc_starts: int32 [512], P(('dp', 'ctx')), parts along dimension 0, may hold values from 0 to 1, as said below
- block_order: int32 [512], P(('dp', 'ctx')), parts along dimension 0, may hold values from 0 to 127, as said below
Outputs:
- packed_out: bfloat16 [65536, 4096], P(('dp', 'ctx')), parts along dimension 0
There are 4 independent parts, one for each index of `dp`. A program takes and returns all parts, laid end to end along the dimension named above; an argument that names none is the same for every part. Nothing has to cross between parts.
Inputs may be any that keep to these rules, and one draw needn't show every extreme that they name: `doc_starts`: block 0 starts a document; no document is longer than 128 blocks. `block_order`: a permutation of the block indices that keeps each document's blocks together and in their order.
All inputs are finite; a program needn't handle non-finite values.
Results may differ from a plain program's by a relative error of at most 0.0085.
Values may be sent and summed in bfloat16 or wider, within the bound.
A program may use at most 128 MiB of HBM per device.

v0:
```python
import jax
import jax.numpy as jnp
from jax import lax
from jax.sharding import PartitionSpec as P

HEAD_DIM = 64
GROUP = 128


def product(form, left, right):
    if left.dtype == jnp.bfloat16 and right.dtype == jnp.bfloat16:
        return jnp.einsum(form, left, right, preferred_element_type=jnp.float32)
    return jnp.einsum(form, left.astype(jnp.float32), right)


def link_maps(earlier, current):
    decay_one, state_one = earlier
    decay_two, state_two = current
    return (decay_one * decay_two, decay_two[..., None, None] * state_one + state_two)


def group_terms(inputs, step_size, decay_speed, scores, write_vector, keep_mask, group_size):
    length, local_heads, head_width = inputs.shape
    group_count = length // group_size
    blocked = inputs.reshape(group_count, group_size, local_heads, head_width)
    steps_blocked = step_size.reshape(group_count, group_size, local_heads).transpose(0, 2, 1)
    cumulative = jnp.cumsum(-steps_blocked * decay_speed[None, :, None], axis=2)
    row_labels = lax.broadcasted_iota(jnp.int32, (group_size, group_size), 0)
    col_ids = lax.broadcasted_iota(jnp.int32, (group_size, group_size), 1)
    gap_log = cumulative[:, :, :, None] - cumulative[:, :, None, :]
    decays = jnp.exp(jnp.where(row_labels >= col_ids, gap_log, -jnp.inf))
    weight = (scores[:, None, :, :] * decays * steps_blocked[:, :, None, :]).astype(jnp.bfloat16)
    local_out = product("chij,cjhp->cihp", weight, blocked)
    last_cum = cumulative[:, :, -1]
    tail_decay = jnp.exp(last_cum[:, :, None] - cumulative) * steps_blocked
    scaled = (blocked.astype(jnp.float32) * tail_decay.transpose(0, 2, 1)[..., None]).astype(
        jnp.bfloat16
    )
    write_blocked = write_vector.reshape(group_count, group_size, -1)
    states = product("cjhp,cjn->chpn", scaled, write_blocked)
    factor = jnp.exp(last_cum) * keep_mask[:, None]
    scan_decay, scan_state = lax.associative_scan(link_maps, (factor, states))
    return (local_out, cumulative, scan_decay, scan_state)


def finish_groups(
    local_out,
    cumulative,
    scan_decay,
    scan_state,
    keep_mask,
    read_vector,
    starting_entry,
    inputs,
    skip_gain,
):
    group_count, group_size, local_heads, head_width = local_out.shape
    prior_decay = jnp.concatenate([jnp.ones((1, local_heads), jnp.float32), scan_decay[:-1]], 0)
    prior_state = jnp.concatenate(
        [jnp.zeros((1,) + scan_state.shape[1:], jnp.float32), scan_state[:-1]], 0
    )
    entering = keep_mask[:, None, None, None] * (
        prior_decay[:, :, None, None] * starting_entry[None] + prior_state
    )
    read_blocked = read_vector.reshape(group_count, group_size, -1)
    carried = product("cin,chpn->cihp", read_blocked, entering)
    carried = carried * jnp.exp(cumulative).transpose(0, 2, 1)[..., None]
    blocked = inputs.reshape(local_out.shape).astype(jnp.float32)
    result = local_out + carried + skip_gain[None, None, :, None] * blocked
    return result.reshape(group_count * group_size, local_heads * head_width)


def gated_norm(gated, norm_weight):
    values = gated.astype(jnp.float32)
    mean_square = jnp.mean(values * values, axis=-1, keepdims=True)
    return (values * lax.rsqrt(mean_square + 1e-05) * norm_weight).astype(jnp.bfloat16)


def route_owners(values, all_order):
    block_count = all_order.shape[0]
    regrouped = values.reshape(block_count, -1, values.shape[1])[all_order].reshape(values.shape)
    return lax.all_to_all(regrouped, "ctx", split_axis=0, concat_axis=1, tiled=True)


def group_scores(read_vector, write_vector):
    group_count = read_vector.shape[0] // GROUP
    return product(
        "cin,cjn->cij",
        read_vector.reshape(group_count, GROUP, -1),
        write_vector.reshape(group_count, GROUP, -1),
    )


def local(
    head_input,
    gate_input,
    write_vector,
    read_vector,
    increment_preactivation,
    step_bias,
    decay_log,
    skip_gain,
    norm_weight,
    doc_starts,
    block_order,
):
    ctx_devices = lax.axis_size("ctx")
    local_heads = step_bias.shape[0] // ctx_devices
    head_start = lax.axis_index("ctx") * local_heads
    moved_input, moved_gate, moved_logit = (
        lax.all_to_all(head_input, "ctx", split_axis=1, concat_axis=0, tiled=True),
        lax.all_to_all(gate_input, "ctx", split_axis=1, concat_axis=0, tiled=True),
        lax.all_to_all(increment_preactivation, "ctx", split_axis=1, concat_axis=0, tiled=True),
    )
    all_write, all_read = (
        lax.all_gather(write_vector, "ctx", axis=0, tiled=True),
        lax.all_gather(read_vector, "ctx", axis=0, tiled=True),
    )
    all_starts, all_order = (
        lax.all_gather(doc_starts, "ctx", axis=0, tiled=True),
        lax.all_gather(block_order, "ctx", axis=0, tiled=True),
    )
    bias_part = lax.dynamic_slice_in_dim(step_bias, head_start, local_heads)
    rate_part = jnp.exp(lax.dynamic_slice_in_dim(decay_log, head_start, local_heads))
    gain_part = lax.dynamic_slice_in_dim(skip_gain, head_start, local_heads)
    step_size = jax.nn.softplus(moved_logit.astype(jnp.float32) + bias_part[None, :])
    keep_mask = 1.0 - all_starts.astype(jnp.float32)
    inputs = moved_input.reshape(moved_input.shape[0], local_heads, HEAD_DIM)
    scores = group_scores(all_read, all_write)
    local_out, cumulative, scan_decay, scan_state = group_terms(
        inputs, step_size, rate_part, scores, all_write, keep_mask, GROUP
    )
    starting_entry = jnp.zeros((local_heads, HEAD_DIM, all_write.shape[1]), jnp.float32)
    mixed = finish_groups(
        local_out,
        cumulative,
        scan_decay,
        scan_state,
        keep_mask,
        all_read,
        starting_entry,
        inputs,
        gain_part,
    )
    gated = (mixed * jax.nn.silu(moved_gate.astype(jnp.float32))).astype(jnp.bfloat16)
    packed_out = gated_norm(route_owners(gated, all_order), norm_weight)
    return packed_out


def solution(mesh):
    return jax.shard_map(
        local,
        mesh=mesh,
        in_specs=(
            P(("dp", "ctx"), None),
            P(("dp", "ctx"), None),
            P(("dp", "ctx"), None),
            P(("dp", "ctx"), None),
            P(("dp", "ctx"), None),
            P(),
            P(),
            P(),
            P(),
            P(("dp", "ctx")),
            P(("dp", "ctx")),
        ),
        out_specs=P(("dp", "ctx"), None),
        check_vma=False,
    )
```

profile of v0, /device:TPU:1, one launch (start us, length us, event | category | flops | bytes accessed | tf_op | source)
XLA Modules:
  0.0 423.0 jit_solution(15939156148514511774)
XLA Ops:
  6.5 0.7 all-gather.5.cloned.1.call-update
  7.3 0.8 copy.139
  8.6 0.8 reduce.2
  9.4 0.6 reshape.328
  10.0 13.0 %all-to-all-start = ((bf16[64,2,128]{2,1,0:T(2,128)(2,1)}), bf16[64,2,128]{2,1,0:T(2,128)(2,1)S(1)}, u32[]{:S(2)}, u32[]{:S(2)}) async-start(bf16[64,2,128]{2,1,0:T(2,128)(2,1)} %reshape.328), calls=%async_computation | async-start | bytes 65536 | tf_op jit(solution)/shard_map/all_to_all | solution.py:113
  23.1 4.1 copy.117
  27.1 5.2 %all-to-all-done = bf16[64,2,128]{2,1,0:T(2,128)(2,1)S(1)} async-done(((bf16[64,2,128]{2,1,0:T(2,128)(2,1)}), bf16[64,2,128]{2,1,0:T(2,128)(2,1)S(1)}, u32[]{:S(2)}, u32[]{:S(2)}) %all-to-all-start) | async-done | bytes 32800 | tf_op jit(solution)/shard_map/all_to_all | solution.py:113
  32.3 5.3 %all-to-all-start.1 = ((bf16[256,64,64]{0,2,1:T(8,128)(2,1)}), bf16[256,64,64]{0,2,1:T(8,128)(2,1)S(1)}, u32[]{:S(2)}, u32[]{:S(2)}) async-start(bf16[256,64,64]{0,2,1:T(8,128)(2,1)} %bitcast.108), calls=%async_computation.1 | async-start | bytes 4194304 | tf_op jit(solution)/shard_map/all_to_all | solution.py:111
  37.7 0.7 all-gather.3.cloned.1.call-update
  40.8 4.1 copy.125
  46.4 60.0 %all-reduce.31 = (s32[128]{0:T(128)S(1)}, s32[128]{0:T(128)S(1)}) all-reduce(s32[128]{0:T(128)S(1)} %dynamic-update-slice, s32[128]{0:T(128)S(1)} %dynamic-update-slice.1), channel_id=1, replica_groups=mesh['ctx'=64,'dp'=4] {'ctx'}, use_global_device_ids=true, to_apply=%add.29 | all-reduce | flops 256 | bytes 2048
  107.1 9.5 %all-to-all-start.2 = ((bf16[256,64,64]{0,2,1:T(8,128)(2,1)}), bf16[256,64,64]{0,2,1:T(8,128)(2,1)}, u32[]{:S(2)}, u32[]{:S(2)}) async-start(bf16[256,64,64]{0,2,1:T(8,128)(2,1)} %bitcast.107), calls=%async_computation.2 | async-start | bytes 4194304 | tf_op jit(solution)/shard_map/all_to_all | solution.py:112
  116.6 0.7 convert_add_fusion
  121.6 0.7 pad_add_fusion.1
  123.7 0.7 pad_maximum_fusion.6
  126.6 0.7 copy.109
  127.5 0.7 copy.116
  128.2 0.7 copy.122
  129.5 2.5 copy.118
  132.0 4.1 reshape.304
  136.1 1.2 convert_multiply_fusion
  137.3 4.5 %copy.123 = f32[64,256,64]{1,0,2:T(8,128)} copy(f32[64,256,64]{1,2,0:T(8,128)S(1)} %convert_multiply_fusion) | data formatting | bytes 8388608 | tf_op jit(solution)/shard_map/mul | solution.py:69
  141.9 4.8 %mul.387 = f32[128,128,1,64]{1,0,3,2:T(8,128)} reshape(f32[64,256,64]{1,0,2:T(8,128)} %copy.123) | data formatting | bytes 8388608 | tf_op jit(solution)/shard_map/mul | solution.py:69
  146.6 27.8 %all-to-all-done.2 = bf16[256,64,64]{0,2,1:T(8,128)(2,1)} async-done(((bf16[256,64,64]{0,2,1:T(8,128)(2,1)}), bf16[256,64,64]{0,2,1:T(8,128)(2,1)}, u32[]{:S(2)}, u32[]{:S(2)}) %all-to-all-start.2) | async-done | bytes 2097184 | tf_op jit(solution)/shard_map/all_to_all | solution.py:112
  174.5 2.2 convert_bitcast_fusion
  176.7 4.5 %copy.126 = f32[64,256,64]{1,0,2:T(8,128)} copy(f32[64,256,64]{1,2,0:T(8,128)S(1)} %convert_bitcast_fusion) | data formatting | bytes 8388608 | tf_op jit(solution)/shard_map/convert_element_type | solution.py:145
  181.1 4.7 %reshape.307 = f32[128,128,64]{1,0,2:T(8,128)} reshape(f32[64,256,64]{1,0,2:T(8,128)} %copy.126) | data formatting | bytes 8388608 | tf_op jit(solution)/shard_map/convert_element_type | solution.py:145
  185.9 2.3 multiply_convert_fusion.2
  188.2 4.5 %fusion.19 = f32[128,64,128]{2,1,0:T(8,128)S(1)} fusion(bf16[128,128,128]{2,1,0:T(8,128)(2,1)} %bitcast.109, bf16[128,128,64]{1,0,2:T(8,128)(2,1)S(1)} %multiply_convert_fusion.2), kind=kOutput, calls=%fused_computation.27 | convolution fusion | flops 268435456 | bytes 10485760 | tf_op jit(solution)/shard_map/cjhp,cjn->chpn/dot_general | solution.py:12
  193.0 0.9 slice.288
  194.1 0.7 copy-done
  194.8 1.0 copy-done.2
  197.9 0.6 fusion.38
  198.7 0.8 fusion.30
  199.5 0.8 pad_maximum_fusion.4
  200.4 0.8 fusion.29
  201.2 0.8 pad_maximum_fusion.3
  202.1 0.7 copy-done.3
  202.8 0.8 copy-done.4
  203.6 0.9 add.270
  204.6 6.2 %pad.110 = f32[32,1,64,128]{3,2,0,1:T(8,128)S(1)} pad(f32[16,1,64,128]{3,2,0,1:T(8,128)} %add.270, f32[]{:T(128)} %constant.8.clone.1), padding=1_0_1x0_0_0x0_0_0x0_0_0 | pad | bytes 1572868 | tf_op jit(solution)/shard_map/pad | solution.py:42
  210.8 1.4 fusion.28
  212.2 0.9 pad_maximum_fusion.2
  213.1 9.2 %pad.109 = f32[32,1,64,128]{3,2,0,1:T(8,128)} pad(f32[16,1,64,128]{3,2,0,1:T(8,128)} %pad_maximum_fusion.2, f32[]{:T(128)} %constant.8.clone.1), padding=0_1_1x0_0_0x0_0_0x0_0_0 | pad | bytes 1572868 | tf_op jit(solution)/shard_map/pad | solution.py:42
  222.3 2.3 add.272
  224.6 1.4 fusion.27
  226.0 1.0 pad_maximum_fusion.1
  227.1 12.4 %pad.111 = f32[64,1,64,128]{3,2,0,1:T(8,128)S(1)} pad(f32[32,1,64,128]{3,2,0,1:T(8,128)} %pad_maximum_fusion.1, f32[]{:T(128)} %constant.8.clone.1), padding=0_1_1x0_0_0x0_0_0x0_0_0 | pad | bytes 3145732 | tf_op jit(solution)/shard_map/pad | solution.py:42
  239.4 11.2 %pad.112 = f32[64,1,64,128]{3,2,0,1:T(8,128)} pad(f32[32,1,64,128]{3,2,0,1:T(8,128)S(1)} %copy-done.5, f32[]{:T(128)} %constant.8.clone.1), padding=1_0_1x0_0_0x0_0_0x0_0_0 | pad | bytes 3145732 | tf_op jit(solution)/shard_map/pad | solution.py:42
  250.6 3.6 add.274
  254.2 32.1 %pad.187 = f32[128,1,64,128]{3,2,0,1:T(8,128)} pad(f32[64,1,64,128]{3,2,0,1:T(8,128)} %add.274, f32[]{:T(128)} %constant.8.clone.1), padding=1_0_1x0_0_0x0_0_0x0_0_0 | pad | bytes 6291460
  286.3 0.8 slice_bitcast_fusion
  287.0 2.5 fusion.24
  289.7 21.3 %pad.144 = f32[127,1,64,128]{3,2,0,1:T(8,128)} pad(f32[64,1,64,128]{3,2,0,1:T(8,128)S(1)} %pad_maximum_fusion, f32[]{:T(128)} %constant.8.clone.1), padding=0_0_1x0_0_0x0_0_0x0_0_0 | pad | bytes 6258692 | tf_op jit(solution)/shard_map/slice | solution.py:60
  311.0 7.0 %slice_add_fusion.7 = f32[127,1,64,128]{3,2,0,1:T(8,128)} fusion(f32[127,1,64,128]{3,2,0,1:T(8,128)} %pad.144, f32[128,1,64,128]{3,2,0,1:T(8,128)} %pad.187), kind=kLoop, calls=%fused_computation.93 | loop fusion | flops 1040384 | bytes 12484608 | tf_op jit(solution)/shard_map/add | solution.py:42
  318.0 11.3 %fusion = f32[128,128,64]{1,2,0:T(8,128)} fusion(f32[128,128]{1,0:T(8,128)S(1)} %copy-done.9, f32[128,128]{1,0:T(8,128)S(1)} %copy-done.7, pred[128,128]{1,0:T(8,128)(4,1)S(1)} %iota_compare_fusion, bf16[128,128,128]{2,1,0:T(8,128)(2,1)} %bitcast.132, bf16[128,128,128]{2,1,0:T(8,128)(2,1)} %bitcast.110, bf16[128,128,64]{1,0,2:T(8,128)(2,1)S(1)} %copy-done.1), kind=kOutput, calls=%fused_computation.2 | convolution fusion | flops 815792128 | bytes 14827520 | tf_op jit(solution)/shard_map/chij,cjhp->cihp/dot_general | solution.py:12
  329.4 14.6 %fusion.6 = bf16[128,128,64]{1,2,0:T(8,128)(2,1)} fusion(f32[128,128,64]{1,2,0:T(8,128)} %fusion, f32[128,128,1,64]{1,0,3,2:T(8,128)} %mul.387, f32[128,128,64]{1,0,2:T(8,128)} %reshape.307, f32[128,128]{1,0:T(8,128)S(1)} %copy-done.8, bf16[128,128,128]{2,1,0:T(8,128)(2,1)} %bitcast.133, f32[127,1,64,128]{3,2,0,1:T(8,128)} %slice_add_fusion.7, ...), kind=kOutput, calls=%fused_computation.10 | convolution fusion | flops 279969792 | bytes 23102464 | tf_op jit(solution)/shard_map/cin,chpn->cihp/dot_general | solution.py:13
  344.0 2.7 gather_fusion
  346.7 2.7 copy.129
  349.4 2.7 all_to_all.49
  352.0 1.2 copy.130
  353.2 56.5 %all_to_all.55 = bf16[64,256,64]{1,2,0:T(8,128)(2,1)S(1)} all-to-all(bf16[64,256,64]{1,2,0:T(8,128)(2,1)S(1)} %copy.130), channel_id=1, replica_groups=mesh['ctx'=64,'dp'=4] {'ctx'}, dimensions={0} | all-to-all | bytes 4194304 | tf_op jit(solution)/shard_map/all_to_all | solution.py:82
  410.4 1.7 fusion.2
  412.1 4.1 copy.131
  (155 shorter events, 14.4 us)
Async XLA Ops:
  6.5 181.7 %all-gather.5.cloned.1.call-start = ((), (), s32[]{:S(2)}) async-start(), calls=%async_computation.5 | async-start | bytes 4259840 | tf_op jit(solution)/shard_map/all_gather | solution.py:116
  10.0 22.3 %all-to-all-start = ((bf16[64,2,128]{2,1,0:T(2,128)(2,1)}), bf16[64,2,128]{2,1,0:T(2,128)(2,1)S(1)}, u32[]{:S(2)}, u32[]{:S(2)}) async-start(bf16[64,2,128]{2,1,0:T(2,128)(2,1)} %reshape.328), calls=%async_computation | async-start | bytes 65536 | tf_op jit(solution)/shard_map/all_to_all | solution.py:113
  23.0 15.4 %copy-start.20 = (f32[64]{0:T(128)S(1)}, f32[64]{0:T(128)}, u32[]{:S(2)}) copy-start(f32[64]{0:T(128)} %param.16) | copy-start | bytes 772
  23.0 16.0 %copy-start.21 = (f32[64]{0:T(128)S(1)}, f32[64]{0:T(128)}, u32[]{:S(2)}) copy-start(f32[64]{0:T(128)} %param.17) | copy-start | bytes 772
  23.0 17.1 %copy-start.22 = (f32[64]{0:T(128)S(1)}, f32[64]{0:T(128)}, u32[]{:S(2)}) copy-start(f32[64]{0:T(128)} %param.18) | copy-start | bytes 772
  32.3 12.5 %copy-start.25 = (u32[256]{0:T(256)S(1)}, u32[256]{0:T(256)}, u32[]{:S(2)}) copy-start(u32[256]{0:T(256)} %constant.98) | copy-start | bytes 3076
  32.3 13.6 %copy-start.23 = (s32[2]{0:T(128)S(1)}, s32[2]{0:T(128)}, u32[]{:S(2)}) copy-start(s32[2]{0:T(128)} %param.20) | copy-start | bytes 28
  32.3 13.9 %copy-start.24 = (s32[2]{0:T(128)S(1)}, s32[2]{0:T(128)}, u32[]{:S(2)}) copy-start(s32[2]{0:T(128)} %param.21) | copy-start | bytes 28
  32.3 74.8 %all-to-all-start.1 = ((bf16[256,64,64]{0,2,1:T(8,128)(2,1)}), bf16[256,64,64]{0,2,1:T(8,128)(2,1)S(1)}, u32[]{:S(2)}, u32[]{:S(2)}) async-start(bf16[256,64,64]{0,2,1:T(8,128)(2,1)} %bitcast.108), calls=%async_computation.1 | async-start | bytes 4194304 | tf_op jit(solution)/shard_map/all_to_all | solution.py:111
  37.6 280.4 %all-gather.3.cloned.1.call-start = ((), (), s32[]{:S(2)}) async-start(), calls=%async_computation.4 | async-start | bytes 4259840 | tf_op jit(solution)/shard_map/all_gather | solution.py:117
  107.1 67.4 %all-to-all-start.2 = ((bf16[256,64,64]{0,2,1:T(8,128)(2,1)}), bf16[256,64,64]{0,2,1:T(8,128)(2,1)}, u32[]{:S(2)}, u32[]{:S(2)}) async-start(bf16[256,64,64]{0,2,1:T(8,128)(2,1)} %bitcast.107), calls=%async_computation.2 | async-start | bytes 4194304 | tf_op jit(solution)/shard_map/all_to_all | solution.py:112
  119.6 6.8 %copy-start.14 = (f32[3,1]{0,1:T(1,128)}, f32[3,1]{0,1:T(1,128)S(1)}, u32[]{:S(2)}) copy-start(f32[3,1]{0,1:T(1,128)S(1)} %slice.240) | copy-start | bytes 40
  119.7 6.7 %copy-start.13 = (f32[7,1]{0,1:T(1,128)}, f32[7,1]{0,1:T(1,128)S(1)}, u32[]{:S(2)}) copy-start(f32[7,1]{0,1:T(1,128)S(1)} %slice.242) | copy-start | bytes 88
  119.9 6.6 %copy-start.11 = (f32[15,1]{0,1:T(1,128)}, f32[15,1]{0,1:T(1,128)S(1)}, u32[]{:S(2)}) copy-start(f32[15,1]{0,1:T(1,128)S(1)} %slice.244) | copy-start | bytes 184
  125.4 1.1 copy-start.17
  125.6 0.9 copy-start.15
  192.7 2.1 copy-start
  194.8 1.0 copy-start.2
  198.7 12.0 %copy-start.12 = (f32[15,1]{0,1:T(1,128)S(1)}, f32[15,1]{0,1:T(1,128)}, u32[]{:S(2)}) copy-start(f32[15,1]{0,1:T(1,128)} %copy-done.11) | copy-start | bytes 184
  200.4 11.8 %slice-start = ((f32[32,1,64,128]{3,2,0,1:T(8,128)}), f32[1,1,64,128]{3,2,0,1:T(8,128)S(1)}, s32[]{:S(2)}) async-start(f32[32,1,64,128]{3,2,0,1:T(8,128)} %copy-done.2), calls=%async_computation.6 | async-start | bytes 65536 | tf_op jit(solution)/shard_map/slice | solution.py:42
  202.0 0.8 copy-start.3
  202.8 0.8 copy-start.4
  210.8 13.9 %copy-start.18 = (f32[31,1]{0,1:T(1,128)S(1)}, f32[31,1]{0,1:T(1,128)}, u32[]{:S(2)}) copy-start(f32[31,1]{0,1:T(1,128)} %copy-done.17) | copy-start | bytes 376
  213.1 12.9 %copy-start.6 = (f32[1,1,64,128]{3,2,0,1:T(8,128)S(1)}, f32[1,1,64,128]{3,2,0,1:T(8,128)}, u32[]{:S(2)}) copy-start(f32[1,1,64,128]{3,2,0,1:T(8,128)} %slice.288) | copy-start | bytes 98308
  226.0 13.4 %copy-start.5 = (f32[32,1,64,128]{3,2,0,1:T(8,128)S(1)}, f32[32,1,64,128]{3,2,0,1:T(8,128)}, u32[]{:S(2)}) copy-start(f32[32,1,64,128]{3,2,0,1:T(8,128)} %add.272) | copy-start | bytes 3145732
  254.2 32.9 %copy-start.16 = (f32[63,1]{0,1:T(1,128)S(1)}, f32[63,1]{0,1:T(1,128)}, u32[]{:S(2)}) copy-start(f32[63,1]{0,1:T(1,128)} %copy-done.15) | copy-start | bytes 760
  311.0 7.0 %copy-start.1 = (bf16[128,128,64]{1,0,2:T(8,128)(2,1)S(1)}, bf16[128,128,64]{1,0,2:T(8,128)(2,1)}, u32[]{:S(2)}) copy-start(bf16[128,128,64]{1,0,2:T(8,128)(2,1)} %reshape.304) | copy-start | bytes 6291460
  311.0 7.0 %copy-start.7 = (f32[128,128]{1,0:T(8,128)S(1)}, f32[128,128]{1,0:T(8,128)}, u32[]{:S(2)}) copy-start(f32[128,128]{1,0:T(8,128)} %copy.109) | copy-start | bytes 196612
  311.0 7.0 %copy-start.9 = (f32[128,128]{1,0:T(8,128)S(1)}, f32[128,128]{1,0:T(8,128)}, u32[]{:S(2)}) copy-start(f32[128,128]{1,0:T(8,128)} %copy.116) | copy-start | bytes 196612
  318.0 11.4 %copy-start.8 = (f32[128,128]{1,0:T(8,128)S(1)}, f32[128,128]{1,0:T(8,128)}, u32[]{:S(2)}) copy-start(f32[128,128]{1,0:T(8,128)} %copy.122) | copy-start | bytes 196612
  318.0 11.4 %copy-start.19 = (f32[128]{0:T(128)S(1)}, f32[128]{0:T(128)}, u32[]{:S(2)}) copy-start(f32[128]{0:T(128)} %get-tuple-element.14) | copy-start | bytes 1540
  318.0 11.4 %copy-start.26 = (f32[128]{0:T(128)S(1)}, f32[128]{0:T(128)}, u32[]{:S(2)}) copy-start(f32[128]{0:T(128)} %maximum_multiply_fusion) | copy-start | bytes 1540
  353.2 57.2 %copy-start.10 = (f32[4096]{0:T(1024)S(1)}, f32[4096]{0:T(1024)}, u32[]{:S(2)}) copy-start(f32[4096]{0:T(1024)} %param.19) | copy-start | bytes 49156
Sparse Core Ops, SparseCore 0:
  10.1 91.9 all-gather.4
  104.9 81.7 all-gather.2
where the time goes:
time: 431 us; the launch traced here: 423 us
  local copies, waits for them, and re-layouts  157 us (36%)
  blocking collectives  117 us (27%)
  other arithmetic  39.9 us (9%)
  waiting for transfers between devices  34.5 us (8%)
  matrix products  30.5 us (7%)
  starting transfers between devices  27.8 us (6%)
  between operations  17.1 us (4%)
    unnamed x1, blocking collectives  60 us
    all_to_all x1, blocking collectives, route_owners(): lax.all_to_all(regrouped, 'ctx', split_axis=0, concat_axis=1, tiled=True)  56.5 us
    unnamed x65, local copies, waits for them, and re-layouts  45.7 us
    pad x22, local copies, waits for them, and re-layouts, group_terms(): scan_decay, scan_state = lax.associative_scan(link_maps, (factor, states))  40.4 us
    all_to_all x1, waiting for transfers between devices, local(): lax.all_to_all(gate_input, 'ctx', split_axis=1, concat_axis=0, tiled=True)  27.8 us
    slice x1, local copies, waits for them, and re-layouts, finish_groups(): scan_state[:-1]  21.3 us
    dot_general x2, matrix products, product(): return jnp.einsum(form, left, right, preferred_element_type=jnp.float32)  15.8 us
    dot_general x1, matrix products, product(): return jnp.einsum(form, left.astype(jnp.float32), right)  14.6 us
  transfers between devices with their start and end apart: 5, of which 2 were waited for; matrix products, arithmetic and copies ran while one was open for 43% of the time, Pallas kernels for 0%

commit v1 on v0

v1 whole, which is shorter than its diff:
```python
import functools

import jax
import jax.numpy as jnp
from jax import lax
from jax.experimental import pallas as pl
from jax.experimental.pallas import tpu as pltpu
from jax.sharding import PartitionSpec as P

GROUP = 128
HEAD_DIM = 64
STATE = 128
LANES = 128
LOG2E = 1.4426950408889634
F32 = jnp.float32
BF16 = jnp.bfloat16
MESH = pl.DeviceIdType.MESH


def high(v):
    return v.astype(BF16).astype(F32)


def split2(v):
    hi = high(v)
    return hi.astype(BF16), (v - hi).astype(BF16)


def split3(v):
    hi = high(v)
    mid = high(v - hi)
    return hi.astype(BF16), mid.astype(BF16), (v - hi - mid).astype(BF16)


def dot(a, b):
    return jnp.dot(a, b, preferred_element_type=F32)


def iota(shape, dim):
    return lax.broadcasted_iota(jnp.int32, shape, dim)


def picks_two(k):
    shape = (2 * HEAD_DIM, LANES)
    return ((iota(shape, 0) & 63) == 2 * k + (iota(shape, 1) >> 6)).astype(BF16)


def picks_three(k):
    shape = (192, 2 * LANES)
    return ((iota(shape, 0) & 63) == 2 * k + (iota(shape, 1) >> 7)).astype(BF16)


def local_kernel(starts_ref, x_ref, b_ref, c_ref, inc_ref, par_ref,
                 m_ref, s0_ref, f_ref, d_ref, e2_ref, col_s, exp_s, row_s, bt_s, sc_s):
    pairs = x_ref.shape[1] // LANES
    par = par_ref[...]
    bias, rate, skip = par[0:1, :], jnp.exp(par[1:2, :]), par[2:3, :]
    v = inc_ref[...].astype(F32) + bias
    step = jnp.maximum(v, 0.0) + jnp.log(1.0 + jnp.exp(-jnp.abs(v)))
    fall = -step * rate
    tri = (iota((GROUP, GROUP), 0) >= iota((GROUP, GROUP), 1))
    ones = tri.astype(F32)
    logs = []
    decs = []
    for b in range(2):
        rows = slice(b * GROUP, (b + 1) * GROUP)
        st = step[rows, :]
        cum = jnp.dot(ones, fall[rows, :], preferred_element_type=F32, precision=lax.Precision.HIGHEST)
        last = cum[GROUP - 1:GROUP, :]
        keep = 1.0 - starts_ref[b].astype(F32)
        decs.append(keep * jnp.exp(last))
        td = jnp.exp(last - cum) * st
        exp_s[rows, :] = jnp.concatenate(split2(td), axis=1)
        ec = jnp.concatenate(split2(jnp.exp(cum)), axis=1)
        exp_s[pl.ds(256 + b * GROUP, GROUP), :] = ec
        col_s[rows, :] = jnp.concatenate(split3(cum * LOG2E), axis=1)
        logs.append((jnp.log(st) - cum) * LOG2E)
        bb = b_ref[rows, :]
        bt_s[rows, :] = bb.astype(F32).T.astype(BF16)
        sc_s[rows, :] = lax.dot_general(c_ref[rows, :], bb, (((1,), (1,)), ((), ())), preferred_element_type=F32)
    row_s[...] = jnp.concatenate(logs, axis=1).T
    r16 = iota((16, HEAD_DIM), 0)
    small = jnp.where(r16 == 0, decs[0], jnp.where(r16 == 1, decs[1], jnp.where(r16 == 2, skip, 0.0)))
    small = jnp.concatenate(split2(small), axis=1)
    exp_s[pl.ds(512, 16), :] = small
    e2_ref[...] = exp_s[pl.ds(256, 272), :]

    def pair(k, carry):
        lanes = pl.ds(pl.multiple_of(k * LANES, LANES), LANES)
        col = dot(col_s[...], picks_three(k))
        ex = dot(exp_s[...], picks_two(k))
        a0, a1, gain = ex[512:513, :], ex[513:514, :], ex[514:515, :]
        left = iota((GROUP, LANES), 1) < HEAD_DIM
        states = []
        for b in range(2):
            rows = slice(b * GROUP, (b + 1) * GROUP)
            xb = x_ref[rows, lanes]
            xf = xb.astype(F32)
            scaled = (xf * ex[rows, :]).astype(BF16)
            states.append(dot(bt_s[rows, :], scaled))
            outs = []
            for e in range(2):
                gap = col[rows, e * LANES:(e + 1) * LANES] + row_s[pl.ds(b * HEAD_DIM + 2 * k + e, 1), :]
                w = jnp.exp2(jnp.where(tri, gap, -1e30)) * sc_s[rows, :]
                outs.append(dot(w.astype(BF16), xb))
            m_ref[rows, lanes] = (jnp.where(left, outs[0], outs[1]) + gain * xf).astype(BF16)
        s0_ref[:, lanes] = states[0].astype(BF16)
        f_ref[:, lanes] = (a1 * states[0] + states[1]).astype(BF16)
        d_ref[pl.ds(k, 1)] = (a0 * a1).reshape(1, 1, LANES)
        return carry

    lax.fori_loop(0, pairs, pair, 0)


def finish_kernel(starts_ref, g_ref, s0_ref, m_ref, gate_ref, c_ref, e2_ref, out_ref):
    pairs = m_ref.shape[1] // LANES
    keep0 = 1.0 - starts_ref[0].astype(F32)
    keep1 = 1.0 - starts_ref[1].astype(F32)

    def pair(k, carry):
        lanes = pl.ds(pl.multiple_of(k * LANES, LANES), LANES)
        ex = dot(e2_ref[...], picks_two(k))
        g = g_ref[:, lanes].astype(F32)
        after = ex[256:257, :] * g + s0_ref[:, lanes].astype(F32)
        entering = ((keep0 * g).astype(BF16), (keep1 * after).astype(BF16))
        for b in range(2):
            rows = slice(b * GROUP, (b + 1) * GROUP)
            carried = dot(c_ref[rows, :], entering[b])
            mixed = m_ref[rows, lanes].astype(F32) + ex[rows, :] * carried
            z = gate_ref[rows, lanes].astype(F32)
            out_ref[rows, lanes] = (mixed * (z / (1.0 + jnp.exp(-z)))).astype(BF16)
        return carry

    lax.fori_loop(0, pairs, pair, 0)


def greet(n):
    me = lax.axis_index("ctx")
    barrier = pltpu.get_barrier_semaphore()

    def one(t, carry):
        pl.semaphore_signal(barrier, inc=1, device_id={"ctx": lax.rem(me + t, n)}, device_id_type=MESH)
        return carry

    lax.fori_loop(1, n, one, 0)
    pl.semaphore_wait(barrier, n - 1)


def remote(src, dst, send, recv, device):
    return pltpu.make_async_remote_copy(
        src_ref=src, dst_ref=dst, send_sem=send, recv_sem=recv,
        device_id={"ctx": device}, device_id_type=MESH)


def order_of(i, n):
    return jnp.where((i & 1) == 1, (i + 1) // 2, n - i // 2)


def scan_kernel(n, f_ref, d_ref, g_ref, pf, pd, fc, dc, rf, rd, gs, gh, ssem, rsem, bsend, brecv):
    me = lax.axis_index("ctx")
    chip, core = me // 2, me % 2
    chips = n // 2
    other = chip * 2 + (1 - core)
    greet(n)
    swap_f = remote(f_ref, pf, ssem.at[0], rsem.at[0], other)
    swap_d = remote(d_ref, pd, ssem.at[1], rsem.at[1], other)
    swap_f.start()
    swap_d.start()
    swap_f.wait()
    swap_d.wait()
    half = pl.ds(pl.multiple_of(core * 64, 64), 64)
    first = core == 0

    def join(k, carry):
        lanes = pl.ds(pl.multiple_of(k * LANES, LANES), LANES)
        mine, theirs = f_ref[half, lanes].astype(F32), pf[half, lanes].astype(F32)
        dm, dt = d_ref[k], pd[k]
        f0, f1 = jnp.where(first, mine, theirs), jnp.where(first, theirs, mine)
        d1 = jnp.where(first, dt, dm)
        fc[k] = (d1 * f0 + f1).astype(BF16)
        dc[k] = dm * dt
        return carry

    lax.fori_loop(0, chips, join, 0)

    def out_copies(i):
        k = lax.rem(chip + order_of(i, chips), chips)
        return (remote(fc.at[k], rf.at[chip], bsend.at[0, i], brecv.at[0, i], 2 * k + core),
                remote(dc.at[k], rd.at[chip], bsend.at[1, i], brecv.at[1, i], 2 * k + core))

    def each(lo, hi, act):
        def body(i, carry):
            act(i)
            return carry
        lax.fori_loop(lo, hi, body, 0)

    def start_all(make):
        def act(i):
            for copy in make(i):
                copy.start()
        each(1, chips, act)

    def wait_all(make):
        def act(i):
            for copy in make(i):
                copy.wait()
        each(1, chips, act)

    start_all(out_copies)
    rf[chip] = fc[chip]
    rd[chip] = dc[chip]
    wait_all(out_copies)

    def walk(s, g):
        gs[s] = g.astype(BF16)
        return rd[s] * g + rf[s].astype(F32)

    lax.fori_loop(0, chips, walk, jnp.zeros((64, LANES), F32))

    def back_copies(i):
        s = lax.rem(chip + order_of(i, chips), chips)
        return (remote(gs.at[s], gh.at[core, chip], bsend.at[2, i], brecv.at[2, i], 2 * s + core),)

    start_all(back_copies)
    gh[core, chip] = gs[chip]
    wait_all(back_copies)
    swap_g = remote(gh.at[core], gh.at[core], ssem.at[2], rsem.at[2], other)
    swap_g.start()
    swap_g.wait()

    def leave(k, carry):
        lanes = pl.ds(pl.multiple_of(k * LANES, LANES), LANES)
        d0 = pd[k]
        for a in range(2):
            rows = pl.ds(a * 64, 64)
            g = gh[a, k]
            later = (d0 * g.astype(F32) + pf[rows, lanes].astype(F32)).astype(BF16)
            g_ref[rows, lanes] = jnp.where(first, g.astype(F32), later.astype(F32)).astype(BF16)
        return carry

    lax.fori_loop(0, chips, leave, 0)


def route_kernel(n, order_ref, gated_ref, out_ref, buf, perm, send1, recv1, send2, recv2):
    me = lax.axis_index("ctx")
    chip, core = me // 2, me % 2
    greet(n)
    lanes = pl.ds(pl.multiple_of(chip * LANES, LANES), LANES)

    def piece(ref, device):
        k, c = device // 2, device % 2
        return ref.at[:, pl.ds(pl.multiple_of(c * 64, 64), 64), pl.ds(pl.multiple_of(k * LANES, LANES), LANES)]

    def go(i):
        to = lax.rem(me + order_of(i, n), n)
        return remote(piece(gated_ref, to), buf.at[pl.ds(2 * me, 2)], send1.at[i], recv1.at[i], to)

    def back(i):
        to = lax.rem(me + order_of(i, n), n)
        return remote(perm.at[pl.ds(2 * to, 2)], piece(out_ref, me), send2.at[i], recv2.at[i], to)

    def each(act):
        def body(i, carry):
            act(i)
            return carry
        lax.fori_loop(1, n, body, 0)

    each(lambda i: go(i).start())
    rows = pl.ds(pl.multiple_of(core * 64, 64), 64)
    buf[pl.ds(2 * me, 2)] = gated_ref[:, rows, lanes]
    each(lambda i: go(i).wait())

    def pick(q, carry):
        perm[q] = buf[order_ref[q]]
        return carry

    lax.fori_loop(0, 2 * n, pick, 0)
    each(lambda i: back(i).start())
    out_ref[:, rows, lanes] = perm[pl.ds(2 * me, 2)]
    each(lambda i: back(i).wait())


def norm_kernel(v_ref, w_ref, o_ref):
    v = v_ref[...].astype(F32)
    mean = jnp.mean(v * v, axis=-1, keepdims=True)
    o_ref[...] = (v * lax.rsqrt(mean + 1e-05) * w_ref[...]).astype(BF16)


def local(head_input, gate_input, write_vector, read_vector, increment_preactivation, step_bias,
          decay_log, skip_gain, norm_weight, doc_starts, block_order):
    n = lax.axis_size("ctx")
    chips = n // 2
    tokens, width = head_input.shape
    vmem = pl.BlockSpec(memory_space=pltpu.VMEM)
    smem = pl.BlockSpec(memory_space=pltpu.SMEM)
    all_order = lax.all_gather(block_order, "ctx", axis=0, tiled=True)
    par = jnp.zeros((8, HEAD_DIM), F32)
    par = jnp.concatenate([step_bias[None], decay_log[None], skip_gain[None], par[3:]], axis=0)
    m, s0, f, d, e2 = pl.pallas_call(
        local_kernel,
        out_shape=(
            jax.ShapeDtypeStruct((tokens, width), BF16),
            jax.ShapeDtypeStruct((STATE, width), BF16),
            jax.ShapeDtypeStruct((STATE, width), BF16),
            jax.ShapeDtypeStruct((chips, 1, LANES), F32),
            jax.ShapeDtypeStruct((272, 2 * HEAD_DIM), BF16),
        ),
        in_specs=[smem] + [vmem] * 5,
        out_specs=(vmem,) * 5,
        scratch_shapes=[
            pltpu.VMEM((2 * GROUP, 192), BF16),
            pltpu.VMEM((528, 2 * HEAD_DIM), BF16),
            pltpu.VMEM((2 * HEAD_DIM, GROUP), F32),
            pltpu.VMEM((2 * STATE, GROUP), BF16),
            pltpu.VMEM((2 * GROUP, GROUP), F32),
        ],
        name="local_terms",
    )(doc_starts, head_input, write_vector, read_vector, increment_preactivation, par)
    g = pl.pallas_call(
        functools.partial(scan_kernel, n),
        out_shape=jax.ShapeDtypeStruct((STATE, width), BF16),
        in_specs=[vmem] * 2,
        out_specs=vmem,
        scratch_shapes=[
            pltpu.VMEM((STATE, width), BF16),
            pltpu.VMEM((chips, 1, LANES), F32),
            pltpu.VMEM((chips, 64, LANES), BF16),
            pltpu.VMEM((chips, 1, LANES), F32),
            pltpu.VMEM((chips, 64, LANES), BF16),
            pltpu.VMEM((chips, 1, LANES), F32),
            pltpu.VMEM((chips, 64, LANES), BF16),
            pltpu.VMEM((2, chips, 64, LANES), BF16),
            pltpu.SemaphoreType.DMA((3,)),
            pltpu.SemaphoreType.DMA((3,)),
            pltpu.SemaphoreType.DMA((3, chips)),
            pltpu.SemaphoreType.DMA((3, chips)),
        ],
        compiler_params=pltpu.CompilerParams(collective_id=1, has_side_effects=True),
        name="state_scan",
    )(f, d)
    gated = pl.pallas_call(
        finish_kernel,
        out_shape=jax.ShapeDtypeStruct((tokens, width), BF16),
        in_specs=[smem] + [vmem] * 6,
        out_specs=vmem,
        name="finish_terms",
    )(doc_starts, g, s0, m, gate_input, read_vector, e2)
    routed = pl.pallas_call(
        functools.partial(route_kernel, n),
        out_shape=jax.ShapeDtypeStruct((2, GROUP, width), BF16),
        in_specs=[smem, vmem],
        out_specs=vmem,
        scratch_shapes=[
            pltpu.VMEM((2 * n, 64, LANES), BF16),
            pltpu.VMEM((2 * n, 64, LANES), BF16),
        ] + [pltpu.SemaphoreType.DMA((n,))] * 4,
        compiler_params=pltpu.CompilerParams(collective_id=2, has_side_effects=True),
        name="route_blocks",
    )(all_order, gated.reshape(2, GROUP, width))
    return pl.pallas_call(
        norm_kernel,
        out_shape=jax.ShapeDtypeStruct((tokens, width), BF16),
        grid=(8,),
        in_specs=[pl.BlockSpec((tokens // 8, width), lambda i: (i, 0)), pl.BlockSpec((1, width), lambda i: (0, 0))],
        out_specs=pl.BlockSpec((tokens // 8, width), lambda i: (i, 0)),
        name="gated_norm",
    )(routed.reshape(tokens, width), norm_weight[None])


def solution(mesh):
    return jax.shard_map(
        local,
        mesh=mesh,
        in_specs=(
            P(("dp", "ctx"), None),
            P(("dp", "ctx"), None),
            P(("dp", "ctx"), None),
            P(("dp", "ctx"), None),
            P(("dp", "ctx"), None),
            P(),
            P(),
            P(),
            P(),
            P(("dp", "ctx")),
            P(("dp", "ctx")),
        ),
        out_specs=P(("dp", "ctx"), None),
        check_vma=False,
    )
```

time: 431 us -> 219 us (0.51); the launches traced: 423 us -> 218 us
  Pallas kernels: 0 us -> 199 us
  local copies, waits for them, and re-layouts: 157 us -> 2.41 us
  blocking collectives: 117 us -> 14.3 us
  other arithmetic: 39.9 us -> 1.35 us
  waiting for transfers between devices: 34.5 us -> 0 us
  matrix products: 30.5 us -> 0 us
  starting transfers between devices: 27.8 us -> 0 us
  between operations: 17.1 us -> 0.71 us
    pallas_call x0 -> x5, Pallas kernels: none -> 199 us  [the longest x1 112 us: local(): pl.pallas_call(functools.partial(route_kernel, n), out_shape=jax.ShapeDty...]
    all_to_all x1 -> x0, blocking collectives: 56.5 us -> none  [route_owners(): lax.all_to_all(regrouped, 'ctx', split_axis=0, concat_axis=1, tiled=True)]
    unnamed x1, blocking collectives: 60 us -> 14.3 us
    unnamed x65 -> x8, local copies, waits for them, and re-layouts: 45.7 us -> 2.33 us
    pad x22 -> x0, local copies, waits for them, and re-layouts: 40.4 us -> none  [group_terms(): scan_decay, scan_state = lax.associative_scan(link_maps, (factor, states))]
    all_to_all x3 -> x0, waiting for transfers between devices: 33 us -> none  [the longest x1 27.8 us: local(): lax.all_to_all(gate_input, 'ctx', split_axis=1, concat_axis=0, tiled=True)]
    dot_general x3 -> x0, matrix products: 30.5 us -> none  [the longest x2 15.8 us: product(): return jnp.einsum(form, left, right, preferred_element_type=jnp.float32)]
    all_to_all x3 -> x0, starting transfers between devices: 27.8 us -> none  [the longest x1 13 us: local(): lax.all_to_all(increment_preactivation, 'ctx', split_axis=1, concat_axis=...]
  transfers between devices with their start and end apart: 5 -> 0, of which waited for: 2 -> 0; matrix products, arithmetic and copies ran while one was open for 43% -> 0% of each run, Pallas kernels for 0% -> 0%
where the time goes in v1:
time: 219 us; the launch traced here: 218 us
  Pallas kernels  199 us (91%)
  blocking collectives  14.3 us (7%)
  local copies, waits for them, and re-layouts  2.41 us (1%)
    pallas_call x1, Pallas kernels, local(): pl.pallas_call(functools.partial(route_kernel, n), out_shape=jax.ShapeDty...  112 us
    pallas_call x1, Pallas kernels, local(): pl.pallas_call(functools.partial(scan_kernel, n), out_shape=jax.ShapeDtyp...  50.5 us
    pallas_call x1, Pallas kernels, local(): pl.pallas_call(local_kernel, out_shape=(jax.ShapeDtypeStruct((tokens, wid...  16.2 us
    pallas_call x1, Pallas kernels, local(): pl.pallas_call(finish_kernel, out_shape=jax.ShapeDtypeStruct((tokens, wid...  14.3 us
    unnamed x1, blocking collectives  14.3 us
    pallas_call x1, Pallas kernels, local(): pl.pallas_call(norm_kernel, out_shape=jax.ShapeDtypeStruct((tokens, width...  6.18 us

profile of v1, /device:TPU:1, one launch (start us, length us, event | category | flops | bytes accessed | tf_op | source)
XLA Modules:
  0.0 218.2 jit_solution(588781206785772035)
XLA Ops:
  0.0 1.5 copy.12.inc_ref
  1.5 0.1 pad.3.clone
  1.6 1.3 maximum_maximum_fusion.par_ref
  2.9 16.2 %local_terms.1 = (bf16[256,4096]{1,0:T(8,128)(2,1)}, bf16[128,4096]{1,0:T(8,128)(2,1)}, bf16[128,4096]{1,0:T(8,128)(2,1)}, f32[32,1,128]{2,1,0:T(1,128)}, bf16[272,128]{1,0:T(8,128)(2,1)}) custom-call(s32[2]{0:T(128)} %starts_ref.3, bf16[256,4096]{1,0:T(8,128)(2,1)} %x_ref.1, bf16[256,128]{1,0:T(8,128)(2,1)} %b_ref.1, bf16[256,128]{1,0:T(8,128)(2,1)} %c_ref.3, ...), custom_call_target="tpu_custom_call" | custom-call | tf_op jit(solution)/shard_map/local_terms/pallas_call | solution.py:299
  19.1 50.5 %state_scan.1.g_ref = bf16[128,4096]{1,0:T(8,128)(2,1)} custom-call(bf16[128,4096]{1,0:T(8,128)(2,1)} %get-tuple-element.10.f_ref, f32[32,1,128]{2,1,0:T(1,128)} %get-tuple-element.11.d_ref), custom_call_target="tpu_custom_call" | custom-call | tf_op jit(solution)/shard_map/state_scan/pallas_call | solution.py:319
  69.6 0.0 copy-start.1
  69.7 0.0 copy-start
  69.7 14.3 %finish_terms.1 = bf16[256,4096]{1,0:T(8,128)(2,1)} custom-call(s32[2]{0:T(128)} %starts_ref.3, bf16[128,4096]{1,0:T(8,128)(2,1)} %state_scan.1.g_ref, bf16[128,4096]{1,0:T(8,128)(2,1)} %get-tuple-element.12.s0_ref, bf16[256,4096]{1,0:T(8,128)(2,1)} %get-tuple-element.13.m_ref, bf16[256,4096]{1,0:T(8,128)(2,1)} %gate_ref.1, bf16[256,128]{1,0:T(8,128)(2,1)} %c_ref.3, ...), custom_call_target="tpu_custom_call" | custom-call | tf_op jit(solution)/shard_map/finish_terms/pallas_call | solution.py:341
  84.0 0.0 copy-done.1
  84.0 0.6 dynamic-slice
  85.3 0.0 copy-done
  85.3 0.2 dynamic-update-slice
  85.5 14.3 %all-reduce.order_ref = s32[128]{0:T(128)} all-reduce(s32[128]{0:T(128)S(1)} %dynamic-update-slice), channel_id=1, replica_groups=mesh['ctx'=64,'dp'=4] {'ctx'}, use_global_device_ids=true, to_apply=%add | all-reduce | flops 128 | bytes 1024
  99.8 112.2 %route_blocks.1 = bf16[2,128,4096]{2,1,0:T(8,128)(2,1)} custom-call(s32[128]{0:T(128)} %all-reduce.order_ref, bf16[2,128,4096]{2,1,0:T(8,128)(2,1)} %bitcast.8), custom_call_target="tpu_custom_call" | custom-call | tf_op jit(solution)/shard_map/route_blocks/pallas_call | solution.py:348
  212.1 6.2 %gated_norm.1 = bf16[256,4096]{1,0:T(8,128)(2,1)} custom-call(bf16[256,4096]{1,0:T(8,128)(2,1)} %bitcast.7, f32[1,4096]{1,0:T(1,128)} %bitcast.9), custom_call_target="tpu_custom_call" | custom-call | tf_op jit(solution)/shard_map/gated_norm/pallas_call | solution.py:360
  (2 shorter events, 0.0 us)
Async XLA Ops:
  69.6 14.4 %copy-start.1 = (u32[256]{0:T(256)S(1)}, u32[256]{0:T(256)}, u32[]{:S(2)}) copy-start(u32[256]{0:T(256)} %constant.6) | copy-start | bytes 3076
  69.7 15.6 %copy-start = (s32[2]{0:T(128)S(1)}, s32[2]{0:T(128)}, u32[]{:S(2)}) copy-start(s32[2]{0:T(128)} %param.21) | copy-start | bytes 28

commit v2 on v0

v2 whole, which is shorter than its diff:
```python
import functools

import jax
import jax.numpy as jnp
from jax import lax
from jax.experimental import pallas as pl
from jax.experimental.pallas import tpu as pltpu
from jax.sharding import PartitionSpec as P

GROUP = 128
HEAD_DIM = 64
STATE = 128
LANES = 128
LOG2E = 1.4426950408889634
F32 = jnp.float32
BF16 = jnp.bfloat16
MESH = pl.DeviceIdType.MESH


def high(v):
    return v.astype(BF16).astype(F32)


def split2(v):
    hi = high(v)
    return hi.astype(BF16), (v - hi).astype(BF16)


def split3(v):
    hi = high(v)
    mid = high(v - hi)
    return hi.astype(BF16), mid.astype(BF16), (v - hi - mid).astype(BF16)


def dot(a, b):
    return jnp.dot(a, b, preferred_element_type=F32)


def iota(shape, dim):
    return lax.broadcasted_iota(jnp.int32, shape, dim)


def picks_two(k):
    shape = (2 * HEAD_DIM, LANES)
    return ((iota(shape, 0) & 63) == 2 * k + (iota(shape, 1) >> 6)).astype(BF16)


def picks_three(k):
    shape = (192, 2 * LANES)
    return ((iota(shape, 0) & 63) == 2 * k + (iota(shape, 1) >> 7)).astype(BF16)


def remote(src, dst, send, recv, device):
    return pltpu.make_async_remote_copy(
        src_ref=src, dst_ref=dst, send_sem=send, recv_sem=recv,
        device_id={"ctx": device}, device_id_type=MESH)


def order_of(i, n):
    return jnp.where((i & 1) == 1, (i + 1) // 2, n - i // 2)


def each(lo, hi, act, step=1):
    def body(i, carry):
        for u in range(step):
            act(lo + i * step + u)
        return carry

    lax.fori_loop(0, (hi - lo) // step, body, 0)


def mega_kernel(n, starts_ref, mine_ref, x_ref, gate_hbm, b_ref, c_ref, inc_ref, par_ref, out_ref,
                gate_v, m_s, s0_s, f_s, pf, d_s, pd, fc, dc, rf, rd, gs, gh, st1, buf, perm,
                ordrow, ordv, ordsm, col_s, exp_s, row_s, bt_s, sc_s,
                gsem, osem, swf_s, swf_r, swd_s, swd_r, out_sem, back_s, back_r, swg_s, swg_r, one_sem, two_sem):
    me = lax.axis_index("ctx")
    chip, core = me // 2, me % 2
    chips = n // 2
    last = chips - 1
    other = chip * 2 + (1 - core)
    first = core == 0

    def offset(j):
        return jnp.where(j == last, 0, order_of(j + 1, chips))

    def pair_at(j):
        return lax.rem(chip - offset(j) + chips, chips)

    def lanes_of(k):
        return pl.ds(pl.multiple_of(k * LANES, LANES), LANES)

    def half_of(c):
        return pl.ds(pl.multiple_of(c * 64, 64), 64)

    barrier = pltpu.get_barrier_semaphore()
    each(1, n, lambda t: pl.semaphore_signal(
        barrier, inc=1, device_id={"ctx": lax.rem(me + t, n)}, device_id_type=MESH))
    gate_copy = pltpu.make_async_copy(gate_hbm, gate_v, gsem.at[0])
    gate_copy.start()
    lane = iota((1, LANES), 1)
    ordrow[...] = jnp.where(lane == 0, mine_ref[0], mine_ref[1])
    ordv[me] = jnp.where(lane == 0, mine_ref[0], mine_ref[1])

    par = par_ref[...]
    bias, rate, skip = par[0:1, :], jnp.exp(par[1:2, :]), par[2:3, :]
    v = inc_ref[...].astype(F32) + bias
    step = jnp.maximum(v, 0.0) + jnp.log(1.0 + jnp.exp(-jnp.abs(v)))
    fall = -step * rate
    tri = (iota((GROUP, GROUP), 0) >= iota((GROUP, GROUP), 1))
    ones = tri.astype(F32)
    logs, decs = [], []
    keep0 = 1.0 - starts_ref[0].astype(F32)
    keep1 = 1.0 - starts_ref[1].astype(F32)
    for b in range(2):
        rows = slice(b * GROUP, (b + 1) * GROUP)
        st = step[rows, :]
        cum = jnp.dot(ones, fall[rows, :], preferred_element_type=F32, precision=lax.Precision.HIGHEST)
        end = cum[GROUP - 1:GROUP, :]
        decs.append((keep0, keep1)[b] * jnp.exp(end))
        exp_s[rows, :] = jnp.concatenate(split2(jnp.exp(end - cum) * st), axis=1)
        exp_s[pl.ds(256 + b * GROUP, GROUP), :] = jnp.concatenate(split2(jnp.exp(cum)), axis=1)
        col_s[rows, :] = jnp.concatenate(split3(cum * LOG2E), axis=1)
        logs.append((jnp.log(st) - cum) * LOG2E)
        bt_s[rows, :] = b_ref[rows, :].astype(F32).T.astype(BF16)
    r16 = iota((16, HEAD_DIM), 0)
    small = jnp.where(r16 == 0, decs[0], jnp.where(r16 == 1, decs[1], jnp.where(r16 == 2, skip, 0.0)))
    exp_s[pl.ds(512, 16), :] = jnp.concatenate(split2(small), axis=1)

    def states_of(j):
        k = pair_at(j)
        lanes = lanes_of(k)
        pick = picks_two(k)
        ex = dot(exp_s[pl.ds(0, 256), :], pick)
        ends = dot(exp_s[pl.ds(512, 16), :], pick)
        a0, a1 = ends[0:1, :], ends[1:2, :]
        states = []
        for b in range(2):
            rows = slice(b * GROUP, (b + 1) * GROUP)
            scaled = (x_ref[rows, lanes].astype(F32) * ex[rows, :]).astype(BF16)
            states.append(dot(bt_s[rows, :], scaled))
        s0_s[j] = states[0]
        f_s[j] = (a1 * states[0] + states[1]).astype(BF16)
        d_s[j] = a0 * a1

    def swap(q):
        part = pl.ds(q * 8, 8)
        return (remote(f_s.at[part], pf.at[part], swf_s.at[q], swf_r.at[q], other),
                remote(d_s.at[part], pd.at[part], swd_s.at[q], swd_r.at[q], other))

    half = half_of(core)

    def join(j):
        mine, theirs = f_s[j, half, :].astype(F32), pf[j, half, :].astype(F32)
        dm, dt = d_s[j], pd[j]
        f0, f1 = jnp.where(first, mine, theirs), jnp.where(first, theirs, mine)
        fc[j] = (jnp.where(first, dt, dm) * f0 + f1).astype(BF16)
        dc[j] = dm * dt

    def send_state(j):
        to = 2 * pair_at(j) + core
        remote(fc.at[j], rf.at[chip], out_sem.at[0], out_sem.at[1], to).start()
        remote(dc.at[j], rd.at[chip], out_sem.at[2], out_sem.at[3], to).start()

    def join_chunk(q):
        for copy in swap(q):
            copy.wait_recv()
        each(q * 8, q * 8 + 8, join, 2)
        each(q * 8, min(q * 8 + 8, last), send_state)

    for q in range(4):
        each(q * 8, q * 8 + 8, states_of, 2)
        if q == 0:
            pl.semaphore_wait(barrier, n - 1)
        else:
            join_chunk(q - 1)
        for copy in swap(q):
            copy.start()
    each(1, n, lambda t: remote(
        ordrow, ordv.at[me], osem.at[0], osem.at[1], lax.rem(me + t, n)).start())
    row_s[...] = jnp.concatenate(logs, axis=1).T
    for b in range(2):
        rows = slice(b * GROUP, (b + 1) * GROUP)
        sc_s[rows, :] = lax.dot_general(
            c_ref[rows, :], b_ref[rows, :], (((1,), (1,)), ((), ())), preferred_element_type=F32)
    join_chunk(3)
    rf[chip] = fc[last]
    rd[chip] = dc[last]

    def local_of(j):
        k = pair_at(j)
        lanes = lanes_of(k)
        col = dot(col_s[...], picks_three(k))
        gain = dot(exp_s[pl.ds(512, 16), :], picks_two(k))[2:3, :]
        left = iota((GROUP, LANES), 1) < HEAD_DIM
        for b in range(2):
            rows = slice(b * GROUP, (b + 1) * GROUP)
            xb = x_ref[rows, lanes]
            outs = []
            for e in range(2):
                gap = col[rows, e * LANES:(e + 1) * LANES] + row_s[pl.ds(b * HEAD_DIM + 2 * k + e, 1), :]
                w = jnp.exp2(jnp.where(tri, gap, -1e30)) * sc_s[rows, :]
                outs.append(dot(w.astype(BF16), xb))
            m_s[j, rows, :] = jnp.where(left, outs[0], outs[1]) + gain * xb.astype(F32)

    each(0, 16, local_of, 2)
    remote(fc.at[pl.ds(0, last)], rf.at[pl.ds(0, last)], out_sem.at[0], out_sem.at[1], other).wait()
    remote(dc.at[pl.ds(0, last)], rd.at[pl.ds(0, last)], out_sem.at[2], out_sem.at[3], other).wait()

    def walk(s, g):
        gs[s] = g.astype(BF16)
        return rd[s] * g + rf[s].astype(F32)

    lax.fori_loop(0, chips, walk, jnp.zeros((64, LANES), F32))

    def send_back(i):
        s = lax.rem(chip + offset(i), chips)
        remote(gs.at[s], gh.at[core, i], back_s.at[0], back_r.at[i], 2 * s + core).start()

    gh[core, last] = gs[chip]
    each(0, last, send_back)
    each(16, 32, local_of, 2)
    gate_copy.wait()

    def arrived(i):
        remote(gs.at[0], gh.at[core, i], back_s.at[0], back_r.at[i], other).wait_recv()

    def finish(i):
        k = pair_at(i)
        lanes = lanes_of(k)
        pick = picks_two(k)
        ex = dot(exp_s[pl.ds(256, 256), :], pick)
        a0 = dot(exp_s[pl.ds(512, 16), :], pick)[0:1, :]
        g = jnp.concatenate([gh[0, i], gh[1, i]], axis=0).astype(F32)
        g = jnp.where(first, g, pd[i] * g + pf[i].astype(F32))
        after = a0 * g + s0_s[i]
        entering = ((keep0 * g).astype(BF16), (keep1 * after).astype(BF16))
        for b in range(2):
            rows = slice(b * GROUP, (b + 1) * GROUP)
            mixed = m_s[i, rows, :] + ex[rows, :] * dot(c_ref[rows, :], entering[b])
            z = gate_v[rows, lanes].astype(F32)
            st1[i, b] = (mixed * (z / (1.0 + jnp.exp(-z)))).astype(BF16)

    def send_one(i, c):
        remote(st1.at[i, :, half_of(c), :], buf.at[pl.ds(2 * me, 2)],
               one_sem.at[0], one_sem.at[1], 2 * pair_at(i) + c).start()

    def finish_two(t):
        finish(2 * t)
        finish(2 * t + 1)

        @pl.when(t > 0)
        def _():
            for u in range(2):
                for c in range(2):
                    send_one(2 * t - 2 + u, c)

    def swap_back(q):
        part = pl.ds(q * 8, 8)
        return remote(gh.at[core, part], gh.at[core, part], swg_s.at[q], swg_r.at[q], other)

    def swapped(q):
        part = pl.ds(q * 8, 8)
        return remote(gh.at[1 - core, part], gh.at[1 - core, part], swg_s.at[q], swg_r.at[q], other)

    for q in range(4):
        each(q * 8, min(q * 8 + 8, last), arrived)
        swap_back(q).start()
        swapped(q).wait_recv()
        each(q * 4, q * 4 + 4, finish_two)
    buf[pl.ds(2 * me, 2)] = st1[last, :, half, :]
    for q in range(4):
        for copy in swap(q):
            copy.wait_send()
        swap_back(q).wait_send()
    remote(gs.at[pl.ds(0, last)], gs.at[pl.ds(0, last)], back_s.at[0], back_r.at[0], other).wait_send()
    for c in range(2):
        send_one(last - 1, c)
    remote(st1.at[last, :, half_of(1 - core), :], buf.at[pl.ds(2 * me, 2)],
           one_sem.at[0], one_sem.at[1], other).start()
    remote(ordv.at[pl.ds(0, n - 1)], ordv.at[pl.ds(0, n - 1)], osem.at[0], osem.at[1], other).wait()
    to_scalars = pltpu.make_async_copy(ordv, ordsm, gsem.at[1])
    to_scalars.start()
    to_scalars.wait()
    whole = remote(buf.at[pl.ds(0, 2 * n - 2)], buf.at[pl.ds(0, 2 * n - 2)], one_sem.at[0], one_sem.at[1], other)
    whole.wait()

    def pick_at(i):
        to = lax.rem(me + order_of(i, n), n)
        for b in range(2):
            perm[i, b] = buf[ordsm[to, 0, b]]

    def send_two(i):
        to = lax.rem(me + order_of(i, n), n)
        remote(perm.at[i], out_ref.at[:, half, lanes_of(chip)], two_sem.at[0], two_sem.at[1], to).start()

    def pick_and_send(i):
        pick_at(i)

        @pl.when(i > 1)
        def _():
            send_two(i - 1)

    each(1, n, pick_and_send)
    for b in range(2):
        out_ref[b, half, lanes_of(chip)] = buf[ordsm[me, 0, b]]
    send_two(n - 1)
    all_two = remote(perm.at[pl.ds(0, n - 1)], perm.at[pl.ds(0, n - 1)], two_sem.at[0], two_sem.at[1], other)
    all_two.wait()


def norm_kernel(v_ref, w_ref, o_ref):
    v = v_ref[...].astype(F32)
    mean = jnp.mean(v * v, axis=-1, keepdims=True)
    o_ref[...] = (v * lax.rsqrt(mean + 1e-05) * w_ref[...]).astype(BF16)


def local(head_input, gate_input, write_vector, read_vector, increment_preactivation, step_bias,
          decay_log, skip_gain, norm_weight, doc_starts, block_order):
    n = lax.axis_size("ctx")
    chips = n // 2
    tokens, width = head_input.shape
    vmem = pl.BlockSpec(memory_space=pltpu.VMEM)
    smem = pl.BlockSpec(memory_space=pltpu.SMEM)
    par = jnp.concatenate([step_bias[None], decay_log[None], skip_gain[None], jnp.zeros((5, HEAD_DIM), F32)], axis=0)
    dma = pltpu.SemaphoreType.DMA
    routed = pl.pallas_call(
        functools.partial(mega_kernel, n),
        out_shape=jax.ShapeDtypeStruct((2, GROUP, width), BF16),
        in_specs=[smem, smem, vmem, pl.BlockSpec(memory_space=pl.ANY)] + [vmem] * 4,
        out_specs=vmem,
        scratch_shapes=[
            pltpu.VMEM((tokens, width), BF16),
            pltpu.VMEM((chips, tokens, LANES), F32),
            pltpu.VMEM((chips, STATE, LANES), F32),
            pltpu.VMEM((chips, STATE, LANES), BF16),
            pltpu.VMEM((chips, STATE, LANES), BF16),
            pltpu.VMEM((chips, 1, LANES), F32),
            pltpu.VMEM((chips, 1, LANES), F32),
            pltpu.VMEM((chips, 64, LANES), BF16),
            pltpu.VMEM((chips, 1, LANES), F32),
            pltpu.VMEM((chips, 64, LANES), BF16),
            pltpu.VMEM((chips, 1, LANES), F32),
            pltpu.VMEM((chips, 64, LANES), BF16),
            pltpu.VMEM((2, chips, 64, LANES), BF16),
            pltpu.VMEM((chips, 2, GROUP, LANES), BF16),
            pltpu.VMEM((2 * n, 64, LANES), BF16),
            pltpu.VMEM((n, 2, 64, LANES), BF16),
            pltpu.VMEM((1, LANES), jnp.int32),
            pltpu.VMEM((n, 1, LANES), jnp.int32),
            pltpu.SMEM((n, 1, LANES), jnp.int32),
            pltpu.VMEM((2 * GROUP, 192), BF16),
            pltpu.VMEM((528, 2 * HEAD_DIM), BF16),
            pltpu.VMEM((2 * HEAD_DIM, GROUP), F32),
            pltpu.VMEM((2 * STATE, GROUP), BF16),
            pltpu.VMEM((2 * GROUP, GROUP), F32),
            dma((2,)), dma((2,)), dma((4,)), dma((4,)), dma((4,)), dma((4,)), dma((4,)),
            dma((1,)), dma((chips,)), dma((4,)), dma((4,)), dma((2,)), dma((2,)),
        ],
        compiler_params=pltpu.CompilerParams(
            collective_id=1, has_side_effects=True, vmem_limit_bytes=60 * 1024 * 1024),
        name="layer",
    )(doc_starts, block_order, head_input, gate_input, write_vector, read_vector, increment_preactivation, par)
    return pl.pallas_call(
        norm_kernel,
        out_shape=jax.ShapeDtypeStruct((tokens, width), BF16),
        grid=(8,),
        in_specs=[pl.BlockSpec((tokens // 8, width), lambda i: (i, 0)), pl.BlockSpec((1, width), lambda i: (0, 0))],
        out_specs=pl.BlockSpec((tokens // 8, width), lambda i: (i, 0)),
        name="gated_norm",
    )(routed.reshape(tokens, width), norm_weight[None])


def solution(mesh):
    return jax.shard_map(
        local,
        mesh=mesh,
        in_specs=(
            P(("dp", "ctx"), None),
            P(("dp", "ctx"), None),
            P(("dp", "ctx"), None),
            P(("dp", "ctx"), None),
            P(("dp", "ctx"), None),
            P(),
            P(),
            P(),
            P(),
            P(("dp", "ctx")),
            P(("dp", "ctx")),
        ),
        out_specs=P(("dp", "ctx"), None),
        check_vma=False,
    )
```

time: 431 us -> 152 us (0.35); the launches traced: 423 us -> 151 us
  local copies, waits for them, and re-layouts: 157 us -> 1.57 us
  Pallas kernels: 0 us -> 148 us
  blocking collectives: 117 us -> 0 us
  other arithmetic: 39.9 us -> 1.35 us
  waiting for transfers between devices: 34.5 us -> 0 us
  matrix products: 30.5 us -> 0 us
  starting transfers between devices: 27.8 us -> 0 us
  between operations: 17.1 us -> 0.01 us
    pallas_call x0 -> x2, Pallas kernels: none -> 148 us  [the longest x1 141 us: local(): pl.pallas_call(functools.partial(mega_kernel, n), out_shape=jax.ShapeDtyp...]
    unnamed x1 -> x0, blocking collectives: 60 us -> none
    all_to_all x1 -> x0, blocking collectives: 56.5 us -> none  [route_owners(): lax.all_to_all(regrouped, 'ctx', split_axis=0, concat_axis=1, tiled=True)]
    unnamed x65 -> x1, local copies, waits for them, and re-layouts: 45.7 us -> 1.49 us
    pad x22 -> x0, local copies, waits for them, and re-layouts: 40.4 us -> none  [group_terms(): scan_decay, scan_state = lax.associative_scan(link_maps, (factor, states))]
    all_to_all x3 -> x0, waiting for transfers between devices: 33 us -> none  [the longest x1 27.8 us: local(): lax.all_to_all(gate_input, 'ctx', split_axis=1, concat_axis=0, tiled=True)]
    dot_general x3 -> x0, matrix products: 30.5 us -> none  [the longest x2 15.8 us: product(): return jnp.einsum(form, left, right, preferred_element_type=jnp.float32)]
    all_to_all x3 -> x0, starting transfers between devices: 27.8 us -> none  [the longest x1 13 us: local(): lax.all_to_all(increment_preactivation, 'ctx', split_axis=1, concat_axis=...]
  transfers between devices with their start and end apart: 5 -> 0, of which waited for: 2 -> 0; matrix products, arithmetic and copies ran while one was open for 43% -> 0% of each run, Pallas kernels for 0% -> 0%
where the time goes in v2:
time: 152 us; the launch traced here: 151 us
  Pallas kernels  148 us (97%)
  local copies, waits for them, and re-layouts  1.57 us (1%)
    pallas_call x1, Pallas kernels, local(): pl.pallas_call(functools.partial(mega_kernel, n), out_shape=jax.ShapeDtyp...  141 us
    pallas_call x1, Pallas kernels, local(): pl.pallas_call(norm_kernel, out_shape=jax.ShapeDtypeStruct((tokens, width...  6.18 us

profile of v2, /device:TPU:1, one launch (start us, length us, event | category | flops | bytes accessed | tf_op | source)
XLA Modules:
  0.0 150.5 jit_solution(14853370944175901418)
XLA Ops:
  0.0 0.1 pad.3.clone
  0.1 1.4 maximum_maximum_fusion.par_ref
  1.4 1.5 copy.12.inc_ref
  2.9 141.4 %layer.1 = bf16[2,128,4096]{2,1,0:T(8,128)(2,1)} custom-call(s32[2]{0:T(128)} %starts_ref.1, s32[2]{0:T(128)} %mine_ref.1, bf16[256,4096]{1,0:T(8,128)(2,1)} %x_ref.1, bf16[256,4096]{1,0:T(8,128)(2,1)} %gate_hbm.1, bf16[256,128]{1,0:T(8,128)(2,1)} %b_ref.1, bf16[256,128]{1,0:T(8,128)(2,1)} %c_ref.1, bf16[256,64]{1,0:T(8,128)(2,1)} %copy.12.inc_ref, ...), custom_call_target="tpu_custom_call" | custom-call | tf_op jit(solution)/shard_map/layer/pallas_call | solution.py:326
  144.4 6.2 %gated_norm.1 = bf16[256,4096]{1,0:T(8,128)(2,1)} custom-call(bf16[256,4096]{1,0:T(8,128)(2,1)} %bitcast.5, f32[1,4096]{1,0:T(1,128)} %bitcast.6), custom_call_target="tpu_custom_call" | custom-call | tf_op jit(solution)/shard_map/gated_norm/pallas_call | solution.py:363
  (1 shorter events, 0.0 us)

commit v3 on v2

--- a/solution.py
+++ b/solution.py
@@ -69,9 +69,13 @@
     lax.fori_loop(0, (hi - lo) // step, body, 0)
 
 
-def mega_kernel(n, starts_ref, mine_ref, x_ref, gate_hbm, b_ref, c_ref, inc_ref, par_ref, out_ref,
-                gate_v, m_s, s0_s, f_s, pf, d_s, pd, fc, dc, rf, rd, gs, gh, st1, buf, perm,
-                ordrow, ordv, ordsm, col_s, exp_s, row_s, bt_s, sc_s,
+PARTS = 2
+CHUNK = 4
+
+
+def mega_kernel(n, starts_ref, mine_ref, x_hbm, gate_hbm, b_ref, c_ref, inc_ref, bias_ref, decay_ref, skip_ref, out_ref,
+                x_ref, gate_v, m_s, s0_s, f_s, pf, d_s, pd, fc, dc, rf, rd, gs, gh, st1, buf0, buf1, perm,
+                ordrow, ordv, ordsm, col_s, exp_s, row_s, tail_s, bt_s, sc_s,
                 gsem, osem, swf_s, swf_r, swd_s, swd_r, out_sem, back_s, back_r, swg_s, swg_r, one_sem, two_sem):
     me = lax.axis_index("ctx")
     chip, core = me // 2, me % 2
@@ -96,19 +100,20 @@
     each(1, n, lambda t: pl.semaphore_signal(
         barrier, inc=1, device_id={"ctx": lax.rem(me + t, n)}, device_id_type=MESH))
     gate_copy = pltpu.make_async_copy(gate_hbm, gate_v, gsem.at[0])
+    x_copy = pltpu.make_async_copy(x_hbm, x_ref, gsem.at[2])
+    x_copy.start()
     gate_copy.start()
     lane = iota((1, LANES), 1)
     ordrow[...] = jnp.where(lane == 0, mine_ref[0], mine_ref[1])
     ordv[me] = jnp.where(lane == 0, mine_ref[0], mine_ref[1])
 
-    par = par_ref[...]
-    bias, rate, skip = par[0:1, :], jnp.exp(par[1:2, :]), par[2:3, :]
-    v = inc_ref[...].astype(F32) + bias
+    bias, rate, skip = bias_ref[...], jnp.exp(decay_ref[...]), skip_ref[...]
+    v = inc_ref[...].astype(F32).T + bias
     step = jnp.maximum(v, 0.0) + jnp.log(1.0 + jnp.exp(-jnp.abs(v)))
     fall = -step * rate
     tri = (iota((GROUP, GROUP), 0) >= iota((GROUP, GROUP), 1))
     ones = tri.astype(F32)
-    logs, decs = [], []
+    logs, decs, tails = [], [], []
     keep0 = 1.0 - starts_ref[0].astype(F32)
     keep1 = 1.0 - starts_ref[1].astype(F32)
     for b in range(2):
@@ -117,27 +122,32 @@
         cum = jnp.dot(ones, fall[rows, :], preferred_element_type=F32, precision=lax.Precision.HIGHEST)
         end = cum[GROUP - 1:GROUP, :]
         decs.append((keep0, keep1)[b] * jnp.exp(end))
-        exp_s[rows, :] = jnp.concatenate(split2(jnp.exp(end - cum) * st), axis=1)
-        exp_s[pl.ds(256 + b * GROUP, GROUP), :] = jnp.concatenate(split2(jnp.exp(cum)), axis=1)
+        tails.append(jnp.exp(end - cum) * st)
+        exp_s[rows, :] = jnp.concatenate(split2(jnp.exp(cum)), axis=1)
         col_s[rows, :] = jnp.concatenate(split3(cum * LOG2E), axis=1)
         logs.append((jnp.log(st) - cum) * LOG2E)
-        bt_s[rows, :] = b_ref[rows, :].astype(F32).T.astype(BF16)
+        bt_s[rows, :] = b_ref[rows, :].astype(F32).T
     r16 = iota((16, HEAD_DIM), 0)
     small = jnp.where(r16 == 0, decs[0], jnp.where(r16 == 1, decs[1], jnp.where(r16 == 2, skip, 0.0)))
-    exp_s[pl.ds(512, 16), :] = jnp.concatenate(split2(small), axis=1)
+    tail_s[...] = jnp.concatenate(tails, axis=1).T
+    exp_s[pl.ds(256, 16), :] = jnp.concatenate(split2(small), axis=1)
+
+    left = iota((GROUP, LANES), 1) < HEAD_DIM
+    x_copy.wait()
 
     def states_of(j):
         k = pair_at(j)
         lanes = lanes_of(k)
         pick = picks_two(k)
-        ex = dot(exp_s[pl.ds(0, 256), :], pick)
-        ends = dot(exp_s[pl.ds(512, 16), :], pick)
+        ends = dot(exp_s[pl.ds(256, 16), :], pick)
         a0, a1 = ends[0:1, :], ends[1:2, :]
         states = []
         for b in range(2):
             rows = slice(b * GROUP, (b + 1) * GROUP)
-            scaled = (x_ref[rows, lanes].astype(F32) * ex[rows, :]).astype(BF16)
-            states.append(dot(bt_s[rows, :], scaled))
+            both = jnp.concatenate(
+                [bt_s[rows, :] * tail_s[pl.ds(b * HEAD_DIM + 2 * k + e, 1), :] for e in range(2)], axis=0)
+            out = dot(both.astype(BF16), x_ref[rows, lanes])
+            states.append(jnp.where(left, out[:STATE], out[STATE:]))
         s0_s[j] = states[0]
         f_s[j] = (a1 * states[0] + states[1]).astype(BF16)
         d_s[j] = a0 * a1
@@ -190,8 +200,7 @@
         k = pair_at(j)
         lanes = lanes_of(k)
         col = dot(col_s[...], picks_three(k))
-        gain = dot(exp_s[pl.ds(512, 16), :], picks_two(k))[2:3, :]
-        left = iota((GROUP, LANES), 1) < HEAD_DIM
+        gain = dot(exp_s[pl.ds(256, 16), :], picks_two(k))[2:3, :]
         for b in range(2):
             rows = slice(b * GROUP, (b + 1) * GROUP)
             xb = x_ref[rows, lanes]
@@ -228,8 +237,8 @@
         k = pair_at(i)
         lanes = lanes_of(k)
         pick = picks_two(k)
-        ex = dot(exp_s[pl.ds(256, 256), :], pick)
-        a0 = dot(exp_s[pl.ds(512, 16), :], pick)[0:1, :]
+        ex = dot(exp_s[...], pick)
+        a0 = ex[256:257, :]
         g = jnp.concatenate([gh[0, i], gh[1, i]], axis=0).astype(F32)
         g = jnp.where(first, g, pd[i] * g + pf[i].astype(F32))
         after = a0 * g + s0_s[i]
@@ -240,9 +249,19 @@
             z = gate_v[rows, lanes].astype(F32)
             st1[i, b] = (mixed * (z / (1.0 + jnp.exp(-z)))).astype(BF16)
 
-    def send_one(i, c):
-        remote(st1.at[i, :, half_of(c), :], buf.at[pl.ds(2 * me, 2)],
-               one_sem.at[0], one_sem.at[1], 2 * pair_at(i) + c).start()
+    size = 64 // PARTS
+    bufs = (buf0, buf1)
+
+    def cut(c, p):
+        return pl.ds(pl.multiple_of(c * 64 + p * size, size), size)
+
+    def send_one(i, c, p):
+        remote(st1.at[i, :, cut(c, p), :], bufs[p].at[pl.ds(2 * me, 2)],
+               one_sem.at[0, p], one_sem.at[1, p], 2 * pair_at(i) + c).start()
+
+    def send_last(p):
+        remote(st1.at[last, :, cut(1 - core, p), :], bufs[p].at[pl.ds(2 * me, 2)],
+               one_sem.at[0, p], one_sem.at[1, p], other).start()
 
     def finish_two(t):
         finish(2 * t)
@@ -252,66 +271,99 @@
         def _():
             for u in range(2):
                 for c in range(2):
-                    send_one(2 * t - 2 + u, c)
+                    send_one(2 * t - 2 + u, c, 0)
 
     def swap_back(q):
-        part = pl.ds(q * 8, 8)
+        part = pl.ds(q * CHUNK, CHUNK)
         return remote(gh.at[core, part], gh.at[core, part], swg_s.at[q], swg_r.at[q], other)
 
     def swapped(q):
-        part = pl.ds(q * 8, 8)
+        part = pl.ds(q * CHUNK, CHUNK)
         return remote(gh.at[1 - core, part], gh.at[1 - core, part], swg_s.at[q], swg_r.at[q], other)
 
-    for q in range(4):
-        each(q * 8, min(q * 8 + 8, last), arrived)
-        swap_back(q).start()
-        swapped(q).wait_recv()
-        each(q * 4, q * 4 + 4, finish_two)
-    buf[pl.ds(2 * me, 2)] = st1[last, :, half, :]
+    rounds = chips // CHUNK
+    for q in range(rounds + 1):
+        if q < rounds:
+            each(q * CHUNK, min(q * CHUNK + CHUNK, last), arrived)
+            swap_back(q).start()
+        if q > 0:
+            swapped(q - 1).wait_recv()
+            each((q - 1) * CHUNK // 2, q * CHUNK // 2, finish_two)
+    for p in range(PARTS):
+        bufs[p][pl.ds(2 * me, 2)] = st1[last, :, cut(core, p), :]
     for q in range(4):
         for copy in swap(q):
             copy.wait_send()
+    for q in range(rounds):
         swap_back(q).wait_send()
     remote(gs.at[pl.ds(0, last)], gs.at[pl.ds(0, last)], back_s.at[0], back_r.at[0], other).wait_send()
     for c in range(2):
-        send_one(last - 1, c)
-    remote(st1.at[last, :, half_of(1 - core), :], buf.at[pl.ds(2 * me, 2)],
-           one_sem.at[0], one_sem.at[1], other).start()
+        send_one(last - 1, c, 0)
+    send_last(0)
+    for p in range(1, PARTS):
+        def rest(i):
+            for c in range(2):
+                send_one(i, c, p)
+
+        each(0, last, rest)
+        send_last(p)
     remote(ordv.at[pl.ds(0, n - 1)], ordv.at[pl.ds(0, n - 1)], osem.at[0], osem.at[1], other).wait()
     to_scalars = pltpu.make_async_copy(ordv, ordsm, gsem.at[1])
     to_scalars.start()
     to_scalars.wait()
-    whole = remote(buf.at[pl.ds(0, 2 * n - 2)], buf.at[pl.ds(0, 2 * n - 2)], one_sem.at[0], one_sem.at[1], other)
-    whole.wait()
-
-    def pick_at(i):
+
+    def send_two(i, p):
         to = lax.rem(me + order_of(i, n), n)
+        remote(perm.at[p, i], out_ref.at[:, cut(core, p), lanes_of(chip)],
+               two_sem.at[0, p], two_sem.at[1, p], to).start()
+
+    for p in range(PARTS):
+        arrivals = remote(bufs[p].at[pl.ds(0, 2 * n - 2)], bufs[p].at[pl.ds(0, 2 * n - 2)],
+                          one_sem.at[0, p], one_sem.at[1, p], other)
+        arrivals.wait()
+
+        def pick_and_send(i):
+            to = lax.rem(me + order_of(i, n), n)
+            for b in range(2):
+                perm[p, i, b] = bufs[p][ordsm[to, 0, b]]
+
+            @pl.when(i > 1)
+            def _():
+                send_two(i - 1, p)
+
+        each(1, n, pick_and_send)
         for b in range(2):
-            perm[i, b] = buf[ordsm[to, 0, b]]
-
-    def send_two(i):
-        to = lax.rem(me + order_of(i, n), n)
-        remote(perm.at[i], out_ref.at[:, half, lanes_of(chip)], two_sem.at[0], two_sem.at[1], to).start()
-
-    def pick_and_send(i):
-        pick_at(i)
-
-        @pl.when(i > 1)
-        def _():
-            send_two(i - 1)
-
-    each(1, n, pick_and_send)
-    for b in range(2):
-        out_ref[b, half, lanes_of(chip)] = buf[ordsm[me, 0, b]]
-    send_two(n - 1)
-    all_two = remote(perm.at[pl.ds(0, n - 1)], perm.at[pl.ds(0, n - 1)], two_sem.at[0], two_sem.at[1], other)
-    all_two.wait()
-
-
-def norm_kernel(v_ref, w_ref, o_ref):
-    v = v_ref[...].astype(F32)
-    mean = jnp.mean(v * v, axis=-1, keepdims=True)
-    o_ref[...] = (v * lax.rsqrt(mean + 1e-05) * w_ref[...]).astype(BF16)
+            out_ref[b, cut(core, p), lanes_of(chip)] = bufs[p][ordsm[me, 0, b]]
+        send_two(n - 1, p)
+    for p in range(PARTS):
+        remote(perm.at[p, pl.ds(0, n - 1)], perm.at[p, pl.ds(0, n - 1)],
+               two_sem.at[0, p], two_sem.at[1, p], other).wait()
+
+
+def norm_kernel(v_hbm, w_ref, o_hbm, v_ref, o_v, isem, osem):
+    count = isem.shape[0]
+    size = v_ref.shape[0] // count
+
+    def rows(i):
+        return pl.ds(pl.multiple_of(i * size, size), size)
+
+    def load(i):
+        return pltpu.make_async_copy(v_hbm.at[rows(i)], v_ref.at[rows(i)], isem.at[i])
+
+    def store(i):
+        return pltpu.make_async_copy(o_v.at[rows(i)], o_hbm.at[rows(i)], osem.at[i])
+
+    each(0, count, lambda i: load(i).start())
+
+    def body(i):
+        load(i).wait()
+        v = v_ref[rows(i), :].astype(F32)
+        mean = jnp.mean(v * v, axis=-1, keepdims=True)
+        o_v[rows(i), :] = (v * lax.rsqrt(mean + 1e-05) * w_ref[...]).astype(BF16)
+        store(i).start()
+
+    each(0, count, body)
+    each(0, count, lambda i: store(i).wait())
 
 
 def local(head_input, gate_input, write_vector, read_vector, increment_preactivation, step_bias,
@@ -321,14 +373,14 @@
     tokens, width = head_input.shape
     vmem = pl.BlockSpec(memory_space=pltpu.VMEM)
     smem = pl.BlockSpec(memory_space=pltpu.SMEM)
-    par = jnp.concatenate([step_bias[None], decay_log[None], skip_gain[None], jnp.zeros((5, HEAD_DIM), F32)], axis=0)
     dma = pltpu.SemaphoreType.DMA
     routed = pl.pallas_call(
         functools.partial(mega_kernel, n),
         out_shape=jax.ShapeDtypeStruct((2, GROUP, width), BF16),
-        in_specs=[smem, smem, vmem, pl.BlockSpec(memory_space=pl.ANY)] + [vmem] * 4,
+        in_specs=[smem, smem, pl.BlockSpec(memory_space=pltpu.HBM), pl.BlockSpec(memory_space=pltpu.HBM)] + [vmem] * 6,
         out_specs=vmem,
         scratch_shapes=[
+            pltpu.VMEM((tokens, width), BF16),
             pltpu.VMEM((tokens, width), BF16),
             pltpu.VMEM((chips, tokens, LANES), F32),
             pltpu.VMEM((chips, STATE, LANES), F32),
@@ -343,29 +395,33 @@
             pltpu.VMEM((chips, 64, LANES), BF16),
             pltpu.VMEM((2, chips, 64, LANES), BF16),
             pltpu.VMEM((chips, 2, GROUP, LANES), BF16),
-            pltpu.VMEM((2 * n, 64, LANES), BF16),
-            pltpu.VMEM((n, 2, 64, LANES), BF16),
+            pltpu.VMEM((2 * n, 64 // PARTS, LANES), BF16),
+            pltpu.VMEM((2 * n, 64 // PARTS, LANES), BF16),
+            pltpu.VMEM((PARTS, n, 2, 64 // PARTS, LANES), BF16),
             pltpu.VMEM((1, LANES), jnp.int32),
             pltpu.VMEM((n, 1, LANES), jnp.int32),
             pltpu.SMEM((n, 1, LANES), jnp.int32),
             pltpu.VMEM((2 * GROUP, 192), BF16),
-            pltpu.VMEM((528, 2 * HEAD_DIM), BF16),
+            pltpu.VMEM((272, 2 * HEAD_DIM), BF16),
             pltpu.VMEM((2 * HEAD_DIM, GROUP), F32),
-            pltpu.VMEM((2 * STATE, GROUP), BF16),
+            pltpu.VMEM((2 * HEAD_DIM, GROUP), F32),
+            pltpu.VMEM((2 * STATE, GROUP), F32),
             pltpu.VMEM((2 * GROUP, GROUP), F32),
-            dma((2,)), dma((2,)), dma((4,)), dma((4,)), dma((4,)), dma((4,)), dma((4,)),
-            dma((1,)), dma((chips,)), dma((4,)), dma((4,)), dma((2,)), dma((2,)),
+            dma((3,)), dma((2,)), dma((4,)), dma((4,)), dma((4,)), dma((4,)), dma((4,)),
+            dma((1,)), dma((chips,)), dma((chips // CHUNK,)), dma((chips // CHUNK,)), dma((2, PARTS)), dma((2, PARTS)),
         ],
         compiler_params=pltpu.CompilerParams(
-            collective_id=1, has_side_effects=True, vmem_limit_bytes=60 * 1024 * 1024),
+            collective_id=1, has_side_effects=True, vmem_limit_bytes=58 * 1024 * 1024),
         name="layer",
-    )(doc_starts, block_order, head_input, gate_input, write_vector, read_vector, increment_preactivation, par)
+    )(doc_starts, block_order, head_input, gate_input, write_vector, read_vector, increment_preactivation.T,
+      step_bias[None], decay_log[None], skip_gain[None])
     return pl.pallas_call(
         norm_kernel,
         out_shape=jax.ShapeDtypeStruct((tokens, width), BF16),
-        grid=(8,),
-        in_specs=[pl.BlockSpec((tokens // 8, width), lambda i: (i, 0)), pl.BlockSpec((1, width), lambda i: (0, 0))],
-        out_specs=pl.BlockSpec((tokens // 8, width), lambda i: (i, 0)),
+        in_specs=[pl.BlockSpec(memory_space=pl.ANY), vmem],
+        out_specs=pl.BlockSpec(memory_space=pl.ANY),
+        scratch_shapes=[pltpu.VMEM((tokens, width), BF16)] * 2 + [dma((8,)), dma((8,))],
+        compiler_params=pltpu.CompilerParams(vmem_limit_bytes=58 * 1024 * 1024),
         name="gated_norm",
     )(routed.reshape(tokens, width), norm_weight[None])
 

time: 152 us -> 139 us (0.914); the launches traced: 151 us -> 139 us
  Pallas kernels: 148 us -> 139 us
  local copies, waits for them, and re-layouts: 1.57 us -> 0 us
    pallas_call x1, Pallas kernels: 141 us -> 135 us  [local(): pl.pallas_call(functools.partial(mega_kernel, n), out_shape=jax.ShapeDtyp...]
    pallas_call x1, Pallas kernels: 6.18 us -> 3.9 us  [local(): pl.pallas_call(norm_kernel, out_shape=jax.ShapeDtypeStruct((tokens, width...]
where the time goes in v3:
time: 139 us
  Pallas kernels  139 us (100%)
    pallas_call x1, Pallas kernels, local(): pl.pallas_call(functools.partial(mega_kernel, n), out_shape=jax.ShapeDtyp...  135 us
    pallas_call x1, Pallas kernels, local(): pl.pallas_call(norm_kernel, out_shape=jax.ShapeDtypeStruct((tokens, width...  3.9 us

profile of v3, /device:TPU:1, one launch (start us, length us, event | category | flops | bytes accessed | tf_op | source)
XLA Modules:
  0.0 139.3 jit_solution(15499597561760920548)
XLA Ops:
  0.0 135.4 %layer.1 = bf16[2,128,4096]{2,1,0:T(8,128)(2,1)} custom-call(s32[2]{0:T(128)} %starts_ref.1, s32[2]{0:T(128)} %mine_ref.1, bf16[256,4096]{1,0:T(8,128)(2,1)} %x_hbm.1, bf16[256,4096]{1,0:T(8,128)(2,1)} %gate_hbm.1, bf16[256,128]{1,0:T(8,128)(2,1)} %b_ref.1, bf16[256,128]{1,0:T(8,128)(2,1)} %c_ref.1, bf16[64,256]{1,0:T(8,128)(2,1)} %bitcast.7, ...), custom_call_target="tpu_custom_call" | custom-call | tf_op jit(solution)/shard_map/layer/pallas_call | solution.py:377
  135.4 3.9 %gated_norm.1 = bf16[256,4096]{1,0:T(8,128)(2,1)} custom-call(bf16[256,4096]{1,0:T(8,128)(2,1)} %bitcast.6, f32[1,4096]{1,0:T(1,128)} %bitcast.8), custom_call_target="tpu_custom_call" | custom-call | tf_op jit(solution)/shard_map/gated_norm/pallas_call | solution.py:418

commit v4 on v3

--- a/solution.py
+++ b/solution.py
@@ -56,8 +56,8 @@
         device_id={"ctx": device}, device_id_type=MESH)
 
 
-def order_of(i, n):
-    return jnp.where((i & 1) == 1, (i + 1) // 2, n - i // 2)
+def around(i, n):
+    return jnp.where(i == n - 1, 0, jnp.where((i & 1) == 0, i // 2 + 1, n - (i + 1) // 2))
 
 
 def each(lo, hi, act, step=1):
@@ -70,11 +70,12 @@
 
 
 PARTS = 2
-CHUNK = 4
-
-
-def mega_kernel(n, starts_ref, mine_ref, x_hbm, gate_hbm, b_ref, c_ref, inc_ref, bias_ref, decay_ref, skip_ref, out_ref,
-                x_ref, gate_v, m_s, s0_s, f_s, pf, d_s, pd, fc, dc, rf, rd, gs, gh, st1, buf0, buf1, perm,
+W0, W1 = 12, 22
+CHUNK = 2
+
+
+def mega_kernel(n, starts_hbm, mine_hbm, x_hbm, gate_hbm, b_ref, c_ref, inc_ref, bias_ref, decay_ref, skip_ref, out_ref,
+                starts_ref, mine_ref, x_ref, gate_v, m_s, s0_s, f_s, pf, d_s, pd, fc, dc, rf, rd, gs, gh, st1, buf0, buf1, perm,
                 ordrow, ordv, ordsm, col_s, exp_s, row_s, tail_s, bt_s, sc_s,
                 gsem, osem, swf_s, swf_r, swd_s, swd_r, out_sem, back_s, back_r, swg_s, swg_r, one_sem, two_sem):
     me = lax.axis_index("ctx")
@@ -84,11 +85,14 @@
     other = chip * 2 + (1 - core)
     first = core == 0
 
-    def offset(j):
-        return jnp.where(j == last, 0, order_of(j + 1, chips))
+    def shifted(j, sign):
+        return lax.rem(chip + sign * around(j, chips) + chips, chips)
 
     def pair_at(j):
-        return lax.rem(chip - offset(j) + chips, chips)
+        return shifted(j, -1)
+
+    def device_at(i):
+        return lax.rem(me + around(i, n), n)
 
     def lanes_of(k):
         return pl.ds(pl.multiple_of(k * LANES, LANES), LANES)
@@ -99,10 +103,16 @@
     barrier = pltpu.get_barrier_semaphore()
     each(1, n, lambda t: pl.semaphore_signal(
         barrier, inc=1, device_id={"ctx": lax.rem(me + t, n)}, device_id_type=MESH))
+    small = [pltpu.make_async_copy(starts_hbm, starts_ref, gsem.at[3]),
+             pltpu.make_async_copy(mine_hbm, mine_ref, gsem.at[4])]
+    for copy in small:
+        copy.start()
     gate_copy = pltpu.make_async_copy(gate_hbm, gate_v, gsem.at[0])
     x_copy = pltpu.make_async_copy(x_hbm, x_ref, gsem.at[2])
     x_copy.start()
     gate_copy.start()
+    for copy in small:
+        copy.wait()
     lane = iota((1, LANES), 1)
     ordrow[...] = jnp.where(lane == 0, mine_ref[0], mine_ref[1])
     ordv[me] = jnp.where(lane == 0, mine_ref[0], mine_ref[1])
@@ -157,6 +167,10 @@
         return (remote(f_s.at[part], pf.at[part], swf_s.at[q], swf_r.at[q], other),
                 remote(d_s.at[part], pd.at[part], swd_s.at[q], swd_r.at[q], other))
 
+    def begin(q):
+        for copy in swap(q):
+            copy.start()
+
     half = half_of(core)
 
     def join(j):
@@ -166,25 +180,31 @@
         fc[j] = (jnp.where(first, dt, dm) * f0 + f1).astype(BF16)
         dc[j] = dm * dt
 
-    def send_state(j):
+    def quarter(h):
+        return pl.ds(h * 32, 32)
+
+    def send_state(j, h):
         to = 2 * pair_at(j) + core
-        remote(fc.at[j], rf.at[chip], out_sem.at[0], out_sem.at[1], to).start()
-        remote(dc.at[j], rd.at[chip], out_sem.at[2], out_sem.at[3], to).start()
+        remote(fc.at[j, quarter(h)], rf.at[chip, quarter(h)], out_sem.at[0, h], out_sem.at[1, h], to).start()
+        if h == 0:
+            remote(dc.at[j], rd.at[chip], out_sem.at[0, 2], out_sem.at[1, 2], to).start()
 
     def join_chunk(q):
         for copy in swap(q):
             copy.wait_recv()
         each(q * 8, q * 8 + 8, join, 2)
-        each(q * 8, min(q * 8 + 8, last), send_state)
+        each(q * 8, min(q * 8 + 8, last), lambda j: send_state(j, 0))
 
     for q in range(4):
         each(q * 8, q * 8 + 8, states_of, 2)
-        if q == 0:
+        if q == 1:
             pl.semaphore_wait(barrier, n - 1)
-        else:
-            join_chunk(q - 1)
-        for copy in swap(q):
-            copy.start()
+            begin(0)
+            begin(1)
+        elif q > 1:
+            join_chunk(q - 2)
+            begin(q)
+    join_chunk(2)
     each(1, n, lambda t: remote(
         ordrow, ordv.at[me], osem.at[0], osem.at[1], lax.rem(me + t, n)).start())
     row_s[...] = jnp.concatenate(logs, axis=1).T
@@ -193,6 +213,7 @@
         sc_s[rows, :] = lax.dot_general(
             c_ref[rows, :], b_ref[rows, :], (((1,), (1,)), ((), ())), preferred_element_type=F32)
     join_chunk(3)
+    each(0, last, lambda j: send_state(j, 1))
     rf[chip] = fc[last]
     rd[chip] = dc[last]
 
@@ -211,27 +232,37 @@
                 outs.append(dot(w.astype(BF16), xb))
             m_s[j, rows, :] = jnp.where(left, outs[0], outs[1]) + gain * xb.astype(F32)
 
-    each(0, 16, local_of, 2)
-    remote(fc.at[pl.ds(0, last)], rf.at[pl.ds(0, last)], out_sem.at[0], out_sem.at[1], other).wait()
-    remote(dc.at[pl.ds(0, last)], rd.at[pl.ds(0, last)], out_sem.at[2], out_sem.at[3], other).wait()
-
-    def walk(s, g):
-        gs[s] = g.astype(BF16)
-        return rd[s] * g + rf[s].astype(F32)
-
-    lax.fori_loop(0, chips, walk, jnp.zeros((64, LANES), F32))
-
-    def send_back(i):
-        s = lax.rem(chip + offset(i), chips)
-        remote(gs.at[s], gh.at[core, i], back_s.at[0], back_r.at[i], 2 * s + core).start()
-
-    gh[core, last] = gs[chip]
-    each(0, last, send_back)
-    each(16, 32, local_of, 2)
+    def received(h):
+        part = (pl.ds(0, last), quarter(h))
+        remote(fc.at[part], rf.at[part], out_sem.at[0, h], out_sem.at[1, h], other).wait()
+
+    def walk(h):
+        def one(s, g):
+            gs[s, quarter(h), :] = g.astype(BF16)
+            return rd[s] * g + rf[s, quarter(h), :].astype(F32)
+
+        lax.fori_loop(0, chips, one, jnp.zeros((32, LANES), F32))
+        gh[core, last, quarter(h), :] = gs[chip, quarter(h), :]
+
+    def send_back(i, h):
+        s = shifted(i, 1)
+        remote(gs.at[s, quarter(h)], gh.at[core, i, quarter(h)], back_s.at[h], back_r.at[h, i], 2 * s + core).start()
+
+    each(0, W0, local_of, 2)
+    remote(dc.at[pl.ds(0, last)], rd.at[pl.ds(0, last)], out_sem.at[0, 2], out_sem.at[1, 2], other).wait()
+    received(0)
+    walk(0)
+    each(0, last, lambda t: send_back(last - 1 - t, 0))
+    each(W0, W1, local_of, 2)
+    received(1)
+    walk(1)
+    each(0, last, lambda t: send_back(last - 1 - t, 1))
+    each(W1, chips, local_of, 2)
     gate_copy.wait()
 
     def arrived(i):
-        remote(gs.at[0], gh.at[core, i], back_s.at[0], back_r.at[i], other).wait_recv()
+        for h in range(2):
+            remote(gs.at[0, quarter(h)], gh.at[core, i, quarter(h)], back_s.at[h], back_r.at[h, i], other).wait_recv()
 
     def finish(i):
         k = pair_at(i)
@@ -264,14 +295,13 @@
                one_sem.at[0, p], one_sem.at[1, p], other).start()
 
     def finish_two(t):
+        finish(2 * t + 1)
         finish(2 * t)
-        finish(2 * t + 1)
-
-        @pl.when(t > 0)
-        def _():
-            for u in range(2):
+        for u in (3, 2):
+            @pl.when(2 * t + u < last)
+            def _():
                 for c in range(2):
-                    send_one(2 * t - 2 + u, c, 0)
+                    send_one(2 * t + u, c, 0)
 
     def swap_back(q):
         part = pl.ds(q * CHUNK, CHUNK)
@@ -282,13 +312,13 @@
         return remote(gh.at[1 - core, part], gh.at[1 - core, part], swg_s.at[q], swg_r.at[q], other)
 
     rounds = chips // CHUNK
-    for q in range(rounds + 1):
-        if q < rounds:
+    for q in range(rounds - 1, -2, -1):
+        if q >= 0:
             each(q * CHUNK, min(q * CHUNK + CHUNK, last), arrived)
             swap_back(q).start()
-        if q > 0:
-            swapped(q - 1).wait_recv()
-            each((q - 1) * CHUNK // 2, q * CHUNK // 2, finish_two)
+        if q < rounds - 1:
+            swapped(q + 1).wait_recv()
+            each(0, CHUNK // 2, lambda t: finish_two((q + 2) * CHUNK // 2 - 1 - t))
     for p in range(PARTS):
         bufs[p][pl.ds(2 * me, 2)] = st1[last, :, cut(core, p), :]
     for q in range(4):
@@ -296,9 +326,12 @@
             copy.wait_send()
     for q in range(rounds):
         swap_back(q).wait_send()
-    remote(gs.at[pl.ds(0, last)], gs.at[pl.ds(0, last)], back_s.at[0], back_r.at[0], other).wait_send()
-    for c in range(2):
-        send_one(last - 1, c, 0)
+    for h in range(2):
+        part = (pl.ds(0, last), quarter(h))
+        remote(gs.at[part], gs.at[part], back_s.at[h], back_r.at[h, 0], other).wait_send()
+    for j in (1, 0):
+        for c in range(2):
+            send_one(j, c, 0)
     send_last(0)
     for p in range(1, PARTS):
         def rest(i):
@@ -313,9 +346,8 @@
     to_scalars.wait()
 
     def send_two(i, p):
-        to = lax.rem(me + order_of(i, n), n)
         remote(perm.at[p, i], out_ref.at[:, cut(core, p), lanes_of(chip)],
-               two_sem.at[0, p], two_sem.at[1, p], to).start()
+               two_sem.at[0, p], two_sem.at[1, p], device_at(i)).start()
 
     for p in range(PARTS):
         arrivals = remote(bufs[p].at[pl.ds(0, 2 * n - 2)], bufs[p].at[pl.ds(0, 2 * n - 2)],
@@ -323,40 +355,34 @@
         arrivals.wait()
 
         def pick_and_send(i):
-            to = lax.rem(me + order_of(i, n), n)
+            to = device_at(i)
             for b in range(2):
                 perm[p, i, b] = bufs[p][ordsm[to, 0, b]]
 
-            @pl.when(i > 1)
+            @pl.when(i > 0)
             def _():
                 send_two(i - 1, p)
 
-        each(1, n, pick_and_send)
+        each(0, n - 1, pick_and_send)
         for b in range(2):
             out_ref[b, cut(core, p), lanes_of(chip)] = bufs[p][ordsm[me, 0, b]]
-        send_two(n - 1, p)
+        send_two(n - 2, p)
     for p in range(PARTS):
         remote(perm.at[p, pl.ds(0, n - 1)], perm.at[p, pl.ds(0, n - 1)],
                two_sem.at[0, p], two_sem.at[1, p], other).wait()
 
 
-def norm_kernel(v_hbm, w_ref, o_hbm, v_ref, o_v, isem, osem):
-    count = isem.shape[0]
+def norm_kernel(v_ref, w_ref, o_hbm, o_v, osem):
+    count = osem.shape[0]
     size = v_ref.shape[0] // count
 
     def rows(i):
         return pl.ds(pl.multiple_of(i * size, size), size)
 
-    def load(i):
-        return pltpu.make_async_copy(v_hbm.at[rows(i)], v_ref.at[rows(i)], isem.at[i])
-
     def store(i):
         return pltpu.make_async_copy(o_v.at[rows(i)], o_hbm.at[rows(i)], osem.at[i])
 
-    each(0, count, lambda i: load(i).start())
-
     def body(i):
-        load(i).wait()
         v = v_ref[rows(i), :].astype(F32)
         mean = jnp.mean(v * v, axis=-1, keepdims=True)
         o_v[rows(i), :] = (v * lax.rsqrt(mean + 1e-05) * w_ref[...]).astype(BF16)
@@ -372,14 +398,16 @@
     chips = n // 2
     tokens, width = head_input.shape
     vmem = pl.BlockSpec(memory_space=pltpu.VMEM)
-    smem = pl.BlockSpec(memory_space=pltpu.SMEM)
+    hbm = pl.BlockSpec(memory_space=pltpu.HBM)
     dma = pltpu.SemaphoreType.DMA
     routed = pl.pallas_call(
         functools.partial(mega_kernel, n),
         out_shape=jax.ShapeDtypeStruct((2, GROUP, width), BF16),
-        in_specs=[smem, smem, pl.BlockSpec(memory_space=pltpu.HBM), pl.BlockSpec(memory_space=pltpu.HBM)] + [vmem] * 6,
+        in_specs=[hbm] * 4 + [vmem] * 6,
         out_specs=vmem,
         scratch_shapes=[
+            pltpu.SMEM((2,), jnp.int32),
+            pltpu.SMEM((2,), jnp.int32),
             pltpu.VMEM((tokens, width), BF16),
             pltpu.VMEM((tokens, width), BF16),
             pltpu.VMEM((chips, tokens, LANES), F32),
@@ -407,21 +435,22 @@
             pltpu.VMEM((2 * HEAD_DIM, GROUP), F32),
             pltpu.VMEM((2 * STATE, GROUP), F32),
             pltpu.VMEM((2 * GROUP, GROUP), F32),
-            dma((3,)), dma((2,)), dma((4,)), dma((4,)), dma((4,)), dma((4,)), dma((4,)),
-            dma((1,)), dma((chips,)), dma((chips // CHUNK,)), dma((chips // CHUNK,)), dma((2, PARTS)), dma((2, PARTS)),
+            dma((5,)), dma((2,)), dma((4,)), dma((4,)), dma((4,)), dma((4,)), dma((2, 3)),
+            dma((2,)), dma((2, chips)), dma((chips // CHUNK,)), dma((chips // CHUNK,)), dma((2, PARTS)), dma((2, PARTS)),
         ],
         compiler_params=pltpu.CompilerParams(
-            collective_id=1, has_side_effects=True, vmem_limit_bytes=58 * 1024 * 1024),
+            collective_id=1, has_side_effects=True, vmem_limit_bytes=40 * 1024 * 1024),
         name="layer",
-    )(doc_starts, block_order, head_input, gate_input, write_vector, read_vector, increment_preactivation.T,
-      step_bias[None], decay_log[None], skip_gain[None])
+    )(*[pltpu.with_memory_space_constraint(v, pltpu.HBM) for v in (
+        doc_starts, block_order, head_input, gate_input, write_vector, read_vector, increment_preactivation.T,
+        step_bias[None], decay_log[None], skip_gain[None])])
     return pl.pallas_call(
         norm_kernel,
         out_shape=jax.ShapeDtypeStruct((tokens, width), BF16),
-        in_specs=[pl.BlockSpec(memory_space=pl.ANY), vmem],
+        in_specs=[vmem, vmem],
         out_specs=pl.BlockSpec(memory_space=pl.ANY),
-        scratch_shapes=[pltpu.VMEM((tokens, width), BF16)] * 2 + [dma((8,)), dma((8,))],
-        compiler_params=pltpu.CompilerParams(vmem_limit_bytes=58 * 1024 * 1024),
+        scratch_shapes=[pltpu.VMEM((tokens, width), BF16), dma((8,))],
+        compiler_params=pltpu.CompilerParams(vmem_limit_bytes=8 * 1024 * 1024),
         name="gated_norm",
     )(routed.reshape(tokens, width), norm_weight[None])
 

time: 139 us -> 135 us (0.971)
  Pallas kernels: 139 us -> 135 us
    pallas_call x1, Pallas kernels: 135 us -> 132 us  [local(): pl.pallas_call(functools.partial(mega_kernel, n), out_shape=jax.ShapeDtyp...]
    pallas_call x1, Pallas kernels: 3.9 us -> 2.16 us  [local(): pl.pallas_call(norm_kernel, out_shape=jax.ShapeDtypeStruct((tokens, width...]
where the time goes in v4:
time: 135 us
  Pallas kernels  135 us (100%)
    pallas_call x1, Pallas kernels, local(): pl.pallas_call(functools.partial(mega_kernel, n), out_shape=jax.ShapeDtyp...  132 us

profile of v4, /device:TPU:1, one launch (start us, length us, event | category | flops | bytes accessed | tf_op | source)
XLA Modules:
  0.0 134.6 jit_solution(4338451148084046819)
XLA Ops:
  0.0 0.0 copy-start
  0.0 132.4 %layer.1 = bf16[2,128,4096]{2,1,0:T(8,128)(2,1)S(1)} custom-call(s32[2]{0:T(128)} %starts_hbm.1, s32[2]{0:T(128)} %mine_hbm.1, bf16[256,4096]{1,0:T(8,128)(2,1)} %x_hbm.1, bf16[256,4096]{1,0:T(8,128)(2,1)} %gate_hbm.1, bf16[256,128]{1,0:T(8,128)(2,1)} %b_ref.1, bf16[256,128]{1,0:T(8,128)(2,1)} %c_ref.1, bf16[64,256]{1,0:T(8,128)(2,1)} %bitcast.8, ...), custom_call_target="tpu_custom_call" | custom-call | tf_op jit(solution)/shard_map/layer/pallas_call | solution.py:403
  132.4 0.0 copy-done
  132.4 2.2 %gated_norm.1 = bf16[256,4096]{1,0:T(8,128)(2,1)} custom-call(bf16[256,4096]{1,0:T(8,128)(2,1)S(1)} %bitcast.6, f32[1,4096]{1,0:T(1,128)S(1)} %bitcast.7), custom_call_target="tpu_custom_call" | custom-call | tf_op jit(solution)/shard_map/gated_norm/pallas_call | solution.py:447
Async XLA Ops:
  0.0 132.4 %copy-start = (f32[4096]{0:T(1024)S(1)}, f32[4096]{0:T(1024)}, u32[]{:S(2)}) copy-start(f32[4096]{0:T(1024)} %param.19) | copy-start | bytes 49156

commit v5 on v4

--- a/solution.py
+++ b/solution.py
@@ -74,8 +74,8 @@
 CHUNK = 2
 
 
-def mega_kernel(n, starts_hbm, mine_hbm, x_hbm, gate_hbm, b_ref, c_ref, inc_ref, bias_ref, decay_ref, skip_ref, out_ref,
-                starts_ref, mine_ref, x_ref, gate_v, m_s, s0_s, f_s, pf, d_s, pd, fc, dc, rf, rd, gs, gh, st1, buf0, buf1, perm,
+def mega_kernel(n, starts_hbm, mine_hbm, x_hbm, gate_hbm, b_hbm, c_hbm, inc_hbm, bias_hbm, decay_hbm, skip_hbm, out_ref,
+                starts_ref, mine_ref, b_ref, c_ref, inc_ref, bias_ref, decay_ref, skip_ref, cum_s, step_s, x_ref, gate_v, m_s, s0_s, f_s, pf, d_s, pd, fc, dc, rf, rd, gs, gh, st1, buf0, buf1, perm,
                 ordrow, ordv, ordsm, col_s, exp_s, row_s, tail_s, bt_s, sc_s,
                 gsem, osem, swf_s, swf_r, swd_s, swd_r, out_sem, back_s, back_r, swg_s, swg_r, one_sem, two_sem):
     me = lax.axis_index("ctx")
@@ -100,50 +100,51 @@
     def half_of(c):
         return pl.ds(pl.multiple_of(c * 64, 64), 64)
 
+    loads = [pltpu.make_async_copy(src, dst, gsem.at[i]) for i, (src, dst) in enumerate((
+        (inc_hbm, inc_ref), (bias_hbm, bias_ref), (decay_hbm, decay_ref), (b_hbm, b_ref), (starts_hbm, starts_ref),
+        (skip_hbm, skip_ref), (x_hbm, x_ref), (mine_hbm, mine_ref), (c_hbm, c_ref), (gate_hbm, gate_v)))]
+    for copy in loads[:3]:
+        copy.start()
     barrier = pltpu.get_barrier_semaphore()
     each(1, n, lambda t: pl.semaphore_signal(
         barrier, inc=1, device_id={"ctx": lax.rem(me + t, n)}, device_id_type=MESH))
-    small = [pltpu.make_async_copy(starts_hbm, starts_ref, gsem.at[3]),
-             pltpu.make_async_copy(mine_hbm, mine_ref, gsem.at[4])]
-    for copy in small:
+    for copy in loads[3:]:
         copy.start()
-    gate_copy = pltpu.make_async_copy(gate_hbm, gate_v, gsem.at[0])
-    x_copy = pltpu.make_async_copy(x_hbm, x_ref, gsem.at[2])
-    x_copy.start()
-    gate_copy.start()
-    for copy in small:
-        copy.wait()
-    lane = iota((1, LANES), 1)
-    ordrow[...] = jnp.where(lane == 0, mine_ref[0], mine_ref[1])
-    ordv[me] = jnp.where(lane == 0, mine_ref[0], mine_ref[1])
-
-    bias, rate, skip = bias_ref[...], jnp.exp(decay_ref[...]), skip_ref[...]
-    v = inc_ref[...].astype(F32).T + bias
-    step = jnp.maximum(v, 0.0) + jnp.log(1.0 + jnp.exp(-jnp.abs(v)))
-    fall = -step * rate
+
     tri = (iota((GROUP, GROUP), 0) >= iota((GROUP, GROUP), 1))
     ones = tri.astype(F32)
-    logs, decs, tails = [], [], []
+    for copy in loads[:3]:
+        copy.wait()
+    v = inc_ref[...].astype(F32).T + bias_ref[...]
+    step = jnp.maximum(v, 0.0) + jnp.log(1.0 + jnp.exp(-jnp.abs(v)))
+    step_s[...] = step
+    fall = -step * jnp.exp(decay_ref[...])
+    ends, tails = [], []
+    for b in range(2):
+        rows = slice(b * GROUP, (b + 1) * GROUP)
+        cum = jnp.dot(ones, fall[rows, :], preferred_element_type=F32, precision=lax.Precision.HIGHEST)
+        cum_s[rows, :] = cum
+        ends.append(cum[GROUP - 1:GROUP, :])
+        tails.append(jnp.exp(ends[b] - cum) * step[rows, :])
+    tail_s[...] = jnp.concatenate(tails, axis=1).T
+    for copy in loads[3:6]:
+        copy.wait()
     keep0 = 1.0 - starts_ref[0].astype(F32)
     keep1 = 1.0 - starts_ref[1].astype(F32)
     for b in range(2):
         rows = slice(b * GROUP, (b + 1) * GROUP)
-        st = step[rows, :]
-        cum = jnp.dot(ones, fall[rows, :], preferred_element_type=F32, precision=lax.Precision.HIGHEST)
-        end = cum[GROUP - 1:GROUP, :]
-        decs.append((keep0, keep1)[b] * jnp.exp(end))
-        tails.append(jnp.exp(end - cum) * st)
-        exp_s[rows, :] = jnp.concatenate(split2(jnp.exp(cum)), axis=1)
-        col_s[rows, :] = jnp.concatenate(split3(cum * LOG2E), axis=1)
-        logs.append((jnp.log(st) - cum) * LOG2E)
         bt_s[rows, :] = b_ref[rows, :].astype(F32).T
     r16 = iota((16, HEAD_DIM), 0)
-    small = jnp.where(r16 == 0, decs[0], jnp.where(r16 == 1, decs[1], jnp.where(r16 == 2, skip, 0.0)))
-    tail_s[...] = jnp.concatenate(tails, axis=1).T
+    small = jnp.where(r16 == 0, keep0 * jnp.exp(ends[0]), jnp.where(
+        r16 == 1, keep1 * jnp.exp(ends[1]), jnp.where(r16 == 2, skip_ref[...], 0.0)))
     exp_s[pl.ds(256, 16), :] = jnp.concatenate(split2(small), axis=1)
+    loads[7].wait()
+    lane = iota((1, LANES), 1)
+    ordrow[...] = jnp.where(lane == 0, mine_ref[0], mine_ref[1])
+    ordv[me] = jnp.where(lane == 0, mine_ref[0], mine_ref[1])
 
     left = iota((GROUP, LANES), 1) < HEAD_DIM
-    x_copy.wait()
+    loads[6].wait()
 
     def states_of(j):
         k = pair_at(j)
@@ -201,17 +202,23 @@
             pl.semaphore_wait(barrier, n - 1)
             begin(0)
             begin(1)
+            each(1, n, lambda t: remote(
+                ordrow, ordv.at[me], osem.at[0], osem.at[1], lax.rem(me + t, n)).start())
         elif q > 1:
             join_chunk(q - 2)
             begin(q)
     join_chunk(2)
-    each(1, n, lambda t: remote(
-        ordrow, ordv.at[me], osem.at[0], osem.at[1], lax.rem(me + t, n)).start())
-    row_s[...] = jnp.concatenate(logs, axis=1).T
+    loads[8].wait()
+    logs = []
     for b in range(2):
         rows = slice(b * GROUP, (b + 1) * GROUP)
+        cum = cum_s[rows, :]
+        exp_s[rows, :] = jnp.concatenate(split2(jnp.exp(cum)), axis=1)
+        col_s[rows, :] = jnp.concatenate(split3(cum * LOG2E), axis=1)
+        logs.append((jnp.log(step_s[rows, :]) - cum) * LOG2E)
         sc_s[rows, :] = lax.dot_general(
             c_ref[rows, :], b_ref[rows, :], (((1,), (1,)), ((), ())), preferred_element_type=F32)
+    row_s[...] = jnp.concatenate(logs, axis=1).T
     join_chunk(3)
     each(0, last, lambda j: send_state(j, 1))
     rf[chip] = fc[last]
@@ -258,7 +265,7 @@
     walk(1)
     each(0, last, lambda t: send_back(last - 1 - t, 1))
     each(W1, chips, local_of, 2)
-    gate_copy.wait()
+    loads[9].wait()
 
     def arrived(i):
         for h in range(2):
@@ -341,7 +348,7 @@
         each(0, last, rest)
         send_last(p)
     remote(ordv.at[pl.ds(0, n - 1)], ordv.at[pl.ds(0, n - 1)], osem.at[0], osem.at[1], other).wait()
-    to_scalars = pltpu.make_async_copy(ordv, ordsm, gsem.at[1])
+    to_scalars = pltpu.make_async_copy(ordv, ordsm, gsem.at[10])
     to_scalars.start()
     to_scalars.wait()
 
@@ -403,11 +410,19 @@
     routed = pl.pallas_call(
         functools.partial(mega_kernel, n),
         out_shape=jax.ShapeDtypeStruct((2, GROUP, width), BF16),
-        in_specs=[hbm] * 4 + [vmem] * 6,
+        in_specs=[hbm] * 10,
         out_specs=vmem,
         scratch_shapes=[
             pltpu.SMEM((2,), jnp.int32),
             pltpu.SMEM((2,), jnp.int32),
+            pltpu.VMEM((tokens, STATE), BF16),
+            pltpu.VMEM((tokens, STATE), BF16),
+            pltpu.VMEM((HEAD_DIM, tokens), BF16),
+            pltpu.VMEM((1, HEAD_DIM), F32),
+            pltpu.VMEM((1, HEAD_DIM), F32),
+            pltpu.VMEM((1, HEAD_DIM), F32),
+            pltpu.VMEM((tokens, HEAD_DIM), F32),
+            pltpu.VMEM((tokens, HEAD_DIM), F32),
             pltpu.VMEM((tokens, width), BF16),
             pltpu.VMEM((tokens, width), BF16),
             pltpu.VMEM((chips, tokens, LANES), F32),
@@ -435,7 +450,7 @@
             pltpu.VMEM((2 * HEAD_DIM, GROUP), F32),
             pltpu.VMEM((2 * STATE, GROUP), F32),
             pltpu.VMEM((2 * GROUP, GROUP), F32),
-            dma((5,)), dma((2,)), dma((4,)), dma((4,)), dma((4,)), dma((4,)), dma((2, 3)),
+            dma((11,)), dma((2,)), dma((4,)), dma((4,)), dma((4,)), dma((4,)), dma((2, 3)),
             dma((2,)), dma((2, chips)), dma((chips // CHUNK,)), dma((chips // CHUNK,)), dma((2, PARTS)), dma((2, PARTS)),
         ],
         compiler_params=pltpu.CompilerParams(

time: 135 us -> 133 us (0.985)
  Pallas kernels: 135 us -> 133 us
where the time goes in v5:
time: 133 us
  Pallas kernels  133 us (100%)
    pallas_call x1, Pallas kernels, local(): pl.pallas_call(functools.partial(mega_kernel, n), out_shape=jax.ShapeDtyp...  131 us

profile of v5, /device:TPU:1, one launch (start us, length us, event | category | flops | bytes accessed | tf_op | source)
XLA Modules:
  0.0 133.3 jit_solution(17729141896985263515)
XLA Ops:
  0.0 0.0 copy-start
  0.0 131.2 %layer.1 = bf16[2,128,4096]{2,1,0:T(8,128)(2,1)S(1)} custom-call(s32[2]{0:T(128)} %starts_hbm.1, s32[2]{0:T(128)} %mine_hbm.1, bf16[256,4096]{1,0:T(8,128)(2,1)} %x_hbm.1, bf16[256,4096]{1,0:T(8,128)(2,1)} %gate_hbm.1, bf16[256,128]{1,0:T(8,128)(2,1)} %b_hbm.1, bf16[256,128]{1,0:T(8,128)(2,1)} %c_hbm.1, bf16[64,256]{1,0:T(8,128)(2,1)} %bitcast.8, ...), custom_call_target="tpu_custom_call" | custom-call | tf_op jit(solution)/shard_map/layer/pallas_call | solution.py:410
  131.2 0.0 copy-done
  131.2 2.2 %gated_norm.1 = bf16[256,4096]{1,0:T(8,128)(2,1)} custom-call(bf16[256,4096]{1,0:T(8,128)(2,1)S(1)} %bitcast.6, f32[1,4096]{1,0:T(1,128)S(1)} %bitcast.7), custom_call_target="tpu_custom_call" | custom-call | tf_op jit(solution)/shard_map/gated_norm/pallas_call | solution.py:462
Async XLA Ops:
  0.0 131.2 %copy-start = (f32[4096]{0:T(1024)S(1)}, f32[4096]{0:T(1024)}, u32[]{:S(2)}) copy-start(f32[4096]{0:T(1024)} %param.19) | copy-start | bytes 49156

commit v6 on v5

--- a/solution.py
+++ b/solution.py
@@ -69,13 +69,14 @@
     lax.fori_loop(0, (hi - lo) // step, body, 0)
 
 
-PARTS = 2
+SPLIT = (32, 32)
+PARTS = len(SPLIT)
 W0, W1 = 12, 22
 CHUNK = 2
 
 
-def mega_kernel(n, starts_hbm, mine_hbm, x_hbm, gate_hbm, b_hbm, c_hbm, inc_hbm, bias_hbm, decay_hbm, skip_hbm, out_ref,
-                starts_ref, mine_ref, b_ref, c_ref, inc_ref, bias_ref, decay_ref, skip_ref, cum_s, step_s, x_ref, gate_v, m_s, s0_s, f_s, pf, d_s, pd, fc, dc, rf, rd, gs, gh, st1, buf0, buf1, perm,
+def mega_kernel(n, starts_hbm, mine_hbm, x_hbm, gate_hbm, b_hbm, c_hbm, inc_hbm, bias_hbm, decay_hbm, skip_hbm, gain_hbm, out_ref,
+                starts_ref, mine_ref, b_ref, c_ref, inc_ref, bias_ref, decay_ref, skip_ref, gain_ref, cum_s, step_s, x_ref, gate_v, m_s, s0_s, f_s, pf, d_s, pd, fc, dc, rf, rd, gs, gh, st1, buf0, buf1, perm0, perm1,
                 ordrow, ordv, ordsm, col_s, exp_s, row_s, tail_s, bt_s, sc_s,
                 gsem, osem, swf_s, swf_r, swd_s, swd_r, out_sem, back_s, back_r, swg_s, swg_r, one_sem, two_sem):
     me = lax.axis_index("ctx")
@@ -102,7 +103,7 @@
 
     loads = [pltpu.make_async_copy(src, dst, gsem.at[i]) for i, (src, dst) in enumerate((
         (inc_hbm, inc_ref), (bias_hbm, bias_ref), (decay_hbm, decay_ref), (b_hbm, b_ref), (starts_hbm, starts_ref),
-        (skip_hbm, skip_ref), (x_hbm, x_ref), (mine_hbm, mine_ref), (c_hbm, c_ref), (gate_hbm, gate_v)))]
+        (skip_hbm, skip_ref), (x_hbm, x_ref), (mine_hbm, mine_ref), (c_hbm, c_ref), (gate_hbm, gate_v), (gain_hbm, gain_ref)))]
     for copy in loads[:3]:
         copy.start()
     barrier = pltpu.get_barrier_semaphore()
@@ -287,11 +288,10 @@
             z = gate_v[rows, lanes].astype(F32)
             st1[i, b] = (mixed * (z / (1.0 + jnp.exp(-z)))).astype(BF16)
 
-    size = 64 // PARTS
-    bufs = (buf0, buf1)
+    bufs, perms = (buf0, buf1), (perm0, perm1)
 
     def cut(c, p):
-        return pl.ds(pl.multiple_of(c * 64 + p * size, size), size)
+        return pl.ds(pl.multiple_of(c * 64 + sum(SPLIT[:p]), 16), SPLIT[p])
 
     def send_one(i, c, p):
         remote(st1.at[i, :, cut(c, p), :], bufs[p].at[pl.ds(2 * me, 2)],
@@ -348,12 +348,12 @@
         each(0, last, rest)
         send_last(p)
     remote(ordv.at[pl.ds(0, n - 1)], ordv.at[pl.ds(0, n - 1)], osem.at[0], osem.at[1], other).wait()
-    to_scalars = pltpu.make_async_copy(ordv, ordsm, gsem.at[10])
+    to_scalars = pltpu.make_async_copy(ordv, ordsm, gsem.at[11])
     to_scalars.start()
     to_scalars.wait()
 
     def send_two(i, p):
-        remote(perm.at[p, i], out_ref.at[:, cut(core, p), lanes_of(chip)],
+        remote(perms[p].at[i], out_ref.at[:, cut(core, p), lanes_of(chip)],
                two_sem.at[0, p], two_sem.at[1, p], device_at(i)).start()
 
     for p in range(PARTS):
@@ -364,7 +364,7 @@
         def pick_and_send(i):
             to = device_at(i)
             for b in range(2):
-                perm[p, i, b] = bufs[p][ordsm[to, 0, b]]
+                perms[p][i, b] = bufs[p][ordsm[to, 0, b]]
 
             @pl.when(i > 0)
             def _():
@@ -375,28 +375,44 @@
             out_ref[b, cut(core, p), lanes_of(chip)] = bufs[p][ordsm[me, 0, b]]
         send_two(n - 2, p)
     for p in range(PARTS):
-        remote(perm.at[p, pl.ds(0, n - 1)], perm.at[p, pl.ds(0, n - 1)],
-               two_sem.at[0, p], two_sem.at[1, p], other).wait()
-
-
-def norm_kernel(v_ref, w_ref, o_hbm, o_v, osem):
-    count = osem.shape[0]
-    size = v_ref.shape[0] // count
-
-    def rows(i):
-        return pl.ds(pl.multiple_of(i * size, size), size)
+        sent = perms[p].at[pl.ds(0, n - 1)]
+        remote(sent, sent, two_sem.at[0, p], two_sem.at[1, p], other).wait()
+        if p == 0:
+            loads[10].wait()
+
+            def norm_some(i):
+                rows = pl.ds(pl.multiple_of(i % 2 * 64, 64), SPLIT[0])
+                out_ref[i // 2, rows, :] = normed(out_ref[i // 2, rows, :], gain_ref[...])
+
+            each(0, 4, norm_some)
+
+
+def normed(v, gain):
+    v = v.astype(F32)
+    mean = jnp.mean(v * v, axis=-1, keepdims=True)
+    return (v * lax.rsqrt(mean + 1e-05) * gain).astype(BF16)
+
+
+def norm_kernel(v_ref, w_ref, o_hbm, o_v, sem):
+    def done(i):
+        rows = pl.ds(pl.multiple_of(i % 2 * 64, 64), SPLIT[0])
+        return pltpu.make_async_copy(v_ref.at[i // 2, rows], o_hbm.at[i // 2, rows], sem.at[i])
+
+    def late(i):
+        return pl.ds(pl.multiple_of(i % 2 * 64 + SPLIT[0], 16), SPLIT[1])
 
     def store(i):
-        return pltpu.make_async_copy(o_v.at[rows(i)], o_hbm.at[rows(i)], osem.at[i])
+        return pltpu.make_async_copy(o_v.at[i], o_hbm.at[i // 2, late(i)], sem.at[i + 4])
+
+    each(0, 4, lambda i: done(i).start())
 
     def body(i):
-        v = v_ref[rows(i), :].astype(F32)
-        mean = jnp.mean(v * v, axis=-1, keepdims=True)
-        o_v[rows(i), :] = (v * lax.rsqrt(mean + 1e-05) * w_ref[...]).astype(BF16)
+        o_v[i] = normed(v_ref[i // 2, late(i), :], w_ref[...])
         store(i).start()
 
-    each(0, count, body)
-    each(0, count, lambda i: store(i).wait())
+    each(0, 4, body)
+    each(0, 4, lambda i: done(i).wait())
+    each(0, 4, lambda i: store(i).wait())
 
 
 def local(head_input, gate_input, write_vector, read_vector, increment_preactivation, step_bias,
@@ -410,7 +426,7 @@
     routed = pl.pallas_call(
         functools.partial(mega_kernel, n),
         out_shape=jax.ShapeDtypeStruct((2, GROUP, width), BF16),
-        in_specs=[hbm] * 10,
+        in_specs=[hbm] * 11,
         out_specs=vmem,
         scratch_shapes=[
             pltpu.SMEM((2,), jnp.int32),
@@ -421,6 +437,7 @@
             pltpu.VMEM((1, HEAD_DIM), F32),
             pltpu.VMEM((1, HEAD_DIM), F32),
             pltpu.VMEM((1, HEAD_DIM), F32),
+            pltpu.VMEM((1, width), F32),
             pltpu.VMEM((tokens, HEAD_DIM), F32),
             pltpu.VMEM((tokens, HEAD_DIM), F32),
             pltpu.VMEM((tokens, width), BF16),
@@ -438,9 +455,10 @@
             pltpu.VMEM((chips, 64, LANES), BF16),
             pltpu.VMEM((2, chips, 64, LANES), BF16),
             pltpu.VMEM((chips, 2, GROUP, LANES), BF16),
-            pltpu.VMEM((2 * n, 64 // PARTS, LANES), BF16),
-            pltpu.VMEM((2 * n, 64 // PARTS, LANES), BF16),
-            pltpu.VMEM((PARTS, n, 2, 64 // PARTS, LANES), BF16),
+            pltpu.VMEM((2 * n, SPLIT[0], LANES), BF16),
+            pltpu.VMEM((2 * n, SPLIT[1], LANES), BF16),
+            pltpu.VMEM((n, 2, SPLIT[0], LANES), BF16),
+            pltpu.VMEM((n, 2, SPLIT[1], LANES), BF16),
             pltpu.VMEM((1, LANES), jnp.int32),
             pltpu.VMEM((n, 1, LANES), jnp.int32),
             pltpu.SMEM((n, 1, LANES), jnp.int32),
@@ -450,7 +468,7 @@
             pltpu.VMEM((2 * HEAD_DIM, GROUP), F32),
             pltpu.VMEM((2 * STATE, GROUP), F32),
             pltpu.VMEM((2 * GROUP, GROUP), F32),
-            dma((11,)), dma((2,)), dma((4,)), dma((4,)), dma((4,)), dma((4,)), dma((2, 3)),
+            dma((12,)), dma((2,)), dma((4,)), dma((4,)), dma((4,)), dma((4,)), dma((2, 3)),
             dma((2,)), dma((2, chips)), dma((chips // CHUNK,)), dma((chips // CHUNK,)), dma((2, PARTS)), dma((2, PARTS)),
         ],
         compiler_params=pltpu.CompilerParams(
@@ -458,16 +476,17 @@
         name="layer",
     )(*[pltpu.with_memory_space_constraint(v, pltpu.HBM) for v in (
         doc_starts, block_order, head_input, gate_input, write_vector, read_vector, increment_preactivation.T,
-        step_bias[None], decay_log[None], skip_gain[None])])
-    return pl.pallas_call(
+        step_bias[None], decay_log[None], skip_gain[None], norm_weight[None])])
+    out = pl.pallas_call(
         norm_kernel,
-        out_shape=jax.ShapeDtypeStruct((tokens, width), BF16),
+        out_shape=jax.ShapeDtypeStruct((2, GROUP, width), BF16),
         in_specs=[vmem, vmem],
         out_specs=pl.BlockSpec(memory_space=pl.ANY),
-        scratch_shapes=[pltpu.VMEM((tokens, width), BF16), dma((8,))],
+        scratch_shapes=[pltpu.VMEM((4, SPLIT[1], width), BF16), dma((8,))],
         compiler_params=pltpu.CompilerParams(vmem_limit_bytes=8 * 1024 * 1024),
         name="gated_norm",
-    )(routed.reshape(tokens, width), norm_weight[None])
+    )(routed, norm_weight[None])
+    return out.reshape(tokens, width)
 
 
 def solution(mesh):

time: 133 us -> 133 us (level)
  no operation moved by 1% of the time
where the time goes in v6:
time: 133 us
  Pallas kernels  133 us (100%)
    pallas_call x1, Pallas kernels, local(): pl.pallas_call(functools.partial(mega_kernel, n), out_shape=jax.ShapeDtyp...  131 us

profile of v6, /device:TPU:1, one launch (start us, length us, event | category | flops | bytes accessed | tf_op | source)
XLA Modules:
  0.0 132.6 jit_solution(10840639442826317225)
XLA Ops:
  0.0 0.0 copy-start
  0.0 131.1 %layer.1.v_ref = bf16[2,128,4096]{2,1,0:T(8,128)(2,1)S(1)} custom-call(s32[2]{0:T(128)} %starts_hbm.1, s32[2]{0:T(128)} %mine_hbm.1, bf16[256,4096]{1,0:T(8,128)(2,1)} %x_hbm.1, bf16[256,4096]{1,0:T(8,128)(2,1)} %gate_hbm.1, bf16[256,128]{1,0:T(8,128)(2,1)} %b_hbm.1, bf16[256,128]{1,0:T(8,128)(2,1)} %c_hbm.1, bf16[64,256]{1,0:T(8,128)(2,1)} %bitcast.8, ...), custom_call_target="tpu_custom_call" | custom-call | tf_op jit(solution)/shard_map/layer/pallas_call | solution.py:426
  131.1 0.0 copy-done
  131.1 1.5 %gated_norm.1 = bf16[2,128,4096]{2,1,0:T(8,128)(2,1)} custom-call(bf16[2,128,4096]{2,1,0:T(8,128)(2,1)S(1)} %layer.1.v_ref, f32[1,4096]{1,0:T(1,128)S(1)} %bitcast.7), custom_call_target="tpu_custom_call" | custom-call | tf_op jit(solution)/shard_map/gated_norm/pallas_call | solution.py:480
Async XLA Ops:
  0.0 131.1 %copy-start = (f32[4096]{0:T(1024)S(1)}, f32[4096]{0:T(1024)}, u32[]{:S(2)}) copy-start(f32[4096]{0:T(1024)} %param.19) | copy-start | bytes 49156

commit v7 on v6

--- a/solution.py
+++ b/solution.py
@@ -69,6 +69,7 @@
     lax.fori_loop(0, (hi - lo) // step, body, 0)
 
 
+WIDE = 4
 SPLIT = (32, 32)
 PARTS = len(SPLIT)
 W0, W1 = 12, 22
@@ -107,8 +108,20 @@
     for copy in loads[:3]:
         copy.start()
     barrier = pltpu.get_barrier_semaphore()
-    each(1, n, lambda t: pl.semaphore_signal(
-        barrier, inc=1, device_id={"ctx": lax.rem(me + t, n)}, device_id_type=MESH))
+    depth = chips // WIDE
+    x_at, z_at = chip // depth, chip % depth
+
+    def hops(at):
+        return min(at[0], WIDE - at[0]) + min(at[1], depth - at[1])
+
+    def signal(device):
+        pl.semaphore_signal(barrier, inc=1, device_id={"ctx": device}, device_id_type=MESH)
+
+    for dx, dz in sorted(((dx, dz) for dx in range(WIDE) for dz in range(depth)), key=hops, reverse=True)[:last]:
+        peer = 2 * (lax.rem(x_at + dx, WIDE) * depth + lax.rem(z_at + dz, depth))
+        signal(peer)
+        signal(peer + 1)
+    signal(other)
     for copy in loads[3:]:
         copy.start()
 

time: 133 us -> 132 us (level)
  no operation moved by 1% of the time
where the time goes in v7:
time: 132 us
  Pallas kernels  132 us (100%)
    pallas_call x1, Pallas kernels, local(): pl.pallas_call(functools.partial(mega_kernel, n), out_shape=jax.ShapeDtyp...  131 us

profile of v7, /device:TPU:1, one launch (start us, length us, event | category | flops | bytes accessed | tf_op | source)
XLA Modules:
  0.0 132.4 jit_solution(15838716950158323454)
XLA Ops:
  0.0 0.0 copy-start
  0.0 130.8 %layer.1.v_ref = bf16[2,128,4096]{2,1,0:T(8,128)(2,1)S(1)} custom-call(s32[2]{0:T(128)} %starts_hbm.1, s32[2]{0:T(128)} %mine_hbm.1, bf16[256,4096]{1,0:T(8,128)(2,1)} %x_hbm.1, bf16[256,4096]{1,0:T(8,128)(2,1)} %gate_hbm.1, bf16[256,128]{1,0:T(8,128)(2,1)} %b_hbm.1, bf16[256,128]{1,0:T(8,128)(2,1)} %c_hbm.1, bf16[64,256]{1,0:T(8,128)(2,1)} %bitcast.8, ...), custom_call_target="tpu_custom_call" | custom-call | tf_op jit(solution)/shard_map/layer/pallas_call | solution.py:439
  130.8 0.0 copy-done
  130.8 1.5 %gated_norm.1 = bf16[2,128,4096]{2,1,0:T(8,128)(2,1)} custom-call(bf16[2,128,4096]{2,1,0:T(8,128)(2,1)S(1)} %layer.1.v_ref, f32[1,4096]{1,0:T(1,128)S(1)} %bitcast.7), custom_call_target="tpu_custom_call" | custom-call | tf_op jit(solution)/shard_map/gated_norm/pallas_call | solution.py:493
Async XLA Ops:
  0.0 130.8 %copy-start = (f32[4096]{0:T(1024)S(1)}, f32[4096]{0:T(1024)}, u32[]{:S(2)}) copy-start(f32[4096]{0:T(1024)} %param.19) | copy-start | bytes 49156
